TPU v7x, 32 devices: a whole 2x2x4 slice. The times are simulated.
32 devices in a mesh: seq: 16 (over z, x, core), head: 2 (over y).
Axes of the slice: x: 2, y: 2, z: 4, core: 2. Of those that a mesh axis runs over, the one named last changes fastest.
Arguments:
- x_proj: bfloat16 [4096, 8192], P(('seq', 'head')), may hold values from -6 to 6
- z_proj: bfloat16 [4096, 8192], P(('seq', 'head')), may hold values from -6 to 6
- b_proj: bfloat16 [4096, 1024], P(('seq', 'head')), may hold values from -6 to 6
- c_proj: bfloat16 [4096, 1024], P(('seq', 'head')), may hold values from -6 to 6
- dt_raw: bfloat16 [4096, 128], P(('seq', 'head')), may hold values from -3.2 to 3.2, as said below
- dt_bias: float32 [128], P('head'), may hold values from -6.3 to -1.2, as said below
- a_log: float32 [128], P('head'), as said below
- d_skip: float32 [128], P('head'), may hold values from 0.5 to 2
- conv_x: float32 [4, 8192], P(None, 'head'), may hold values from -3 to 3
- conv_bias_x: float32 [8192], P('head'), may hold values from -3 to 3
- conv_bc: float32 [4, 2, 1024], P(None, None, 'head'), may hold values from -3 to 3
- conv_bias_bc: float32 [2, 1024], P(None, 'head'), may hold values from -3 to 3
- norm_weight: float32 [8192], P('head'), may hold values from 0.25 to 1.75
- out_weight: bfloat16 [8192, 4096], P('head', 'seq'), may hold values from -0.0625 to 0.0625
Outputs:
- mixed: bfloat16 [4096, 4096], P(('seq', 'head'))
Inputs may be any that keep to these rules, and one draw needn't show every extreme that they name: `dt_raw`: A normal draw times 0.7 plus an offset common to each head and each aligned run of 256 tokens. `dt_bias`: the inverse softplus of a per-head step size between 0.002 and 0.25. Finite; exp(a_log) lies above 0.0 and at most 0.3.
All inputs are finite; a program needn't handle non-finite values.
Results may differ from a plain program's by a relative error of at most 0.014.
Values may be sent and summed in bfloat16 or wider, within the bound.
A program may use at most 192 MiB of HBM per device.

v0:
```python
import jax
import jax.numpy as jnp
from jax import lax
from jax.sharding import PartitionSpec as P

HEAD_DIM = 64
STATE = 128
GROUPS = 8
SPAN = 128
DI = 8192


def from_behind(array, axis, by):
    count = lax.axis_size(axis)
    pairs = [(i, i + by) for i in range(count) if 0 <= i + by < count]
    return lax.ppermute(array, axis, pairs)


def prefix(value, axis, join, neutral):
    count, mine = (lax.axis_size(axis), lax.axis_index(axis))
    pieces = jax.tree.map(lambda part: lax.all_gather(part, axis), value)
    total = jax.tree.map(
        lambda part, zero: jnp.full_like(part, 0) + jnp.asarray(zero, part.dtype), value, neutral
    )

    def lap(position, total):
        longer = join(total, jax.tree.map(lambda part: part[position], pieces))
        return jax.tree.map(lambda new, old: jnp.where(position < mine, new, old), longer, total)

    return lax.fori_loop(0, count - 1, lap, total)


def depthwise(current, previous, weight, bias_row):
    padded = jnp.concatenate([previous, current], axis=0).astype(jnp.float32)
    token_count = current.shape[0]
    summed = jnp.broadcast_to(bias_row, current.shape)
    for offset in range(weight.shape[0]):
        summed = summed + weight[offset] * padded[offset : offset + token_count]
    return jax.nn.silu(summed).astype(jnp.bfloat16)


def block_weights(c_blocks, b_blocks, cumulative, step_size, per_group):
    scores = jnp.einsum("ktgn,ksgn->kgts", c_blocks, b_blocks, preferred_element_type=jnp.float32)
    by_head = jnp.transpose(cumulative, (0, 2, 1))
    spread = by_head[:, :, :, None] - by_head[:, :, None, :]
    length = cumulative.shape[1]
    causal = jnp.arange(length)[:, None] >= jnp.arange(length)[None, :]
    decays = jnp.exp(jnp.where(causal, spread, -jnp.inf))
    scaled = decays * jnp.transpose(step_size, (0, 2, 1))[:, :, None, :]
    block_count = cumulative.shape[0]
    head_count = cumulative.shape[2]
    grouped = scaled.reshape(block_count, -1, per_group, length, length) * scores[:, :, None]
    return grouped.reshape(block_count, head_count, length, length).astype(jnp.bfloat16)


def combine_states(earlier, later):
    return (earlier[0] + later[0], jnp.exp(later[0])[:, None, None] * earlier[1] + later[1])


def per_device(
    x_proj,
    z_proj,
    b_proj,
    c_proj,
    dt_raw,
    dt_bias,
    a_log,
    d_skip,
    conv_x,
    conv_bias_x,
    conv_bc,
    conv_bias_bc,
    norm_weight,
    out_weight,
):
    x_heads, z_heads, b_heads, c_heads, dt_heads = (
        lax.all_to_all(x_proj, "head", split_axis=1, concat_axis=0, tiled=True),
        lax.all_to_all(z_proj, "head", split_axis=1, concat_axis=0, tiled=True),
        lax.all_to_all(b_proj, "head", split_axis=1, concat_axis=0, tiled=True),
        lax.all_to_all(c_proj, "head", split_axis=1, concat_axis=0, tiled=True),
        lax.all_to_all(dt_raw, "head", split_axis=1, concat_axis=0, tiled=True),
    )
    kernel_len = conv_x.shape[0]
    x_cols = x_heads.shape[1]
    bc_cols = b_heads.shape[1]
    last_rows = jnp.concatenate(
        [x_heads[-(kernel_len - 1) :], b_heads[-(kernel_len - 1) :], c_heads[-(kernel_len - 1) :]],
        axis=1,
    )
    before = from_behind(last_rows, "seq", 1)
    x_conv = depthwise(x_heads, before[:, :x_cols], conv_x, conv_bias_x)
    b_conv = depthwise(
        b_heads, before[:, x_cols : x_cols + bc_cols], conv_bc[:, 0], conv_bias_bc[0]
    )
    c_conv = depthwise(c_heads, before[:, x_cols + bc_cols :], conv_bc[:, 1], conv_bias_bc[1])
    token_count = x_conv.shape[0]
    local_heads = dt_bias.shape[0]
    local_groups = bc_cols // STATE
    per_group = local_heads // local_groups
    blocks = token_count // SPAN
    x_blocks = x_conv.reshape(blocks, SPAN, local_heads, HEAD_DIM)
    b_blocks = b_conv.reshape(blocks, SPAN, local_groups, STATE)
    c_blocks = c_conv.reshape(blocks, SPAN, local_groups, STATE)
    step_size = jax.nn.softplus(dt_heads.astype(jnp.float32) + dt_bias).reshape(
        blocks, SPAN, local_heads
    )
    cumulative = jnp.cumsum(-jnp.exp(a_log) * step_size, axis=1)
    mix_weights = block_weights(c_blocks, b_blocks, cumulative, step_size, per_group)
    y_local = jnp.einsum(
        "khts,kshp->kthp", mix_weights, x_blocks, preferred_element_type=jnp.float32
    )
    state_scale = step_size * jnp.exp(cumulative[:, -1:, :] - cumulative)
    x_weighted = (x_blocks.astype(jnp.float32) * state_scale[:, :, :, None]).astype(jnp.bfloat16)
    x_grouped = x_weighted.reshape(blocks, SPAN, local_groups, per_group, HEAD_DIM)
    pieces = jnp.einsum(
        "ksgqp,ksgn->kgqpn", x_grouped, b_blocks, preferred_element_type=jnp.float32
    )
    pieces = pieces.reshape(blocks, local_heads, HEAD_DIM, STATE)
    totals = cumulative[:, -1, :]
    final_state = jnp.zeros((local_heads, HEAD_DIM, STATE), jnp.float32)
    for block_idx in range(blocks):
        final_state = jnp.exp(totals[block_idx])[:, None, None] * final_state + pieces[block_idx]
    log_total = jnp.sum(totals, axis=0)
    carried = prefix(
        (log_total, final_state),
        "seq",
        combine_states,
        (jnp.zeros_like(log_total), jnp.zeros_like(final_state)),
    )
    running = carried[1]
    start_list = []
    for block_idx in range(blocks):
        start_list.append(running.astype(jnp.bfloat16))
        running = jnp.exp(totals[block_idx])[:, None, None] * running + pieces[block_idx]
    start_states = jnp.stack(start_list).reshape(blocks, local_groups, per_group, HEAD_DIM, STATE)
    y_carry = jnp.einsum(
        "ktgn,kgqpn->ktgqp", c_blocks, start_states, preferred_element_type=jnp.float32
    )
    y_carry = (
        y_carry.reshape(blocks, SPAN, local_heads, HEAD_DIM) * jnp.exp(cumulative)[:, :, :, None]
    )
    outputs = y_local + y_carry + d_skip[:, None] * x_blocks.astype(jnp.float32)
    outputs = outputs.reshape(token_count, local_heads * HEAD_DIM)
    gated = outputs * jax.nn.silu(z_heads.astype(jnp.float32))
    grouped = gated.reshape(token_count, -1, DI // GROUPS)
    normed = grouped / jnp.sqrt(jnp.mean(grouped * grouped, axis=-1, keepdims=True) + 1.0)
    normed = (normed.reshape(token_count, -1) * norm_weight).astype(jnp.bfloat16)
    terms = jnp.dot(
        normed,
        lax.all_gather(out_weight, "seq", axis=1, tiled=True),
        preferred_element_type=jnp.float32,
    )
    mixed = lax.psum_scatter(terms.astype(jnp.bfloat16), "head", scatter_dimension=0, tiled=True)
    return mixed


def solution(mesh):
    in_specs = (
        P(("seq", "head"), None),
        P(("seq", "head"), None),
        P(("seq", "head"), None),
        P(("seq", "head"), None),
        P(("seq", "head"), None),
        P("head"),
        P("head"),
        P("head"),
        P(None, "head"),
        P("head"),
        P(None, None, "head"),
        P(None, "head"),
        P("head"),
        P("head", "seq"),
    )
    out_specs = P(("seq", "head"), None)
    return jax.shard_map(
        per_device, mesh=mesh, in_specs=in_specs, out_specs=out_specs, check_vma=False
    )
```

profile of v0, /device:TPU:8, one launch (start us, length us, event | category | flops | bytes accessed | tf_op | source)
XLA Modules:
  0.0 496.1 jit_solution(14551310706796745205)
XLA Ops:
  6.5 1.5 copy.75
  8.1 3.3 all-to-all-start.3
  11.3 1.7 fusion.53
  13.0 4.1 copy.68
  17.1 0.9 copy.70
  18.0 0.8 copy.72
  18.8 3.4 all-to-all-start.1
  22.9 4.8 all-to-all-done.1
  27.7 3.4 all-to-all-start.2
  31.8 4.6 all-to-all-done.2
  36.3 3.8 all-to-all-start
  42.1 21.0 %all-to-all-done = bf16[128,2,4096]{0,2,1:T(8,128)(2,1)S(1)} async-done(((bf16[128,2,4096]{0,2,1:T(8,128)(2,1)}), bf16[128,2,4096]{0,2,1:T(8,128)(2,1)S(1)}, u32[]{:S(2)}, u32[]{:S(2)}) %all-to-all-start) | async-done | bytes 2097184 | tf_op jit(solution)/shard_map/all_to_all | solution.py:77
  63.2 1.3 copy-done.4
  64.5 2.9 copy.69
  67.5 1.9 collective-permute-start
  70.0 3.7 collective-permute-done
  74.5 1.0 multiply_convert_fusion.7
  75.6 0.8 slice.178
  77.1 2.7 multiply_convert_fusion.4
  79.8 3.1 copy.83
  82.9 5.8 %reshape.168 = f32[2,128,4,16,64]{1,0,4,3,2:T(2,128)} reshape(f32[256,4096]{0,1:T(8,128)} %copy.83) | data formatting | bytes 8388608 | tf_op jit(solution)/shard_map/convert_element_type | solution.py:113
  88.8 4.5 multiply_convert_fusion.3
  93.3 0.7 fusion.22
  94.6 1.3 copy-done
  95.9 1.7 multiply_add_fusion
  97.7 0.7 all-gather.6.cloned.1.call-update
  98.4 2.5 copy.92
  100.9 4.8 all-to-all-start.4
  107.9 24.4 %all-reduce = f32[1024]{0:T(1024)S(1)} all-reduce(f32[1024]{0:T(1024)S(1)} %dynamic-update-slice), channel_id=2, replica_groups=mesh['seq'=16,'head'=2] {'seq'}, use_global_device_ids=true, to_apply=%add | all-reduce | flops 1024 | bytes 8192
  133.1 0.7 copy.79
  133.9 3.8 convert_bitcast_fusion
  137.7 5.7 %copy.93 = f32[2,128,4096]{2,1,0:T(8,128)} copy(f32[2,128,4096]{1,2,0:T(8,128)} %convert_bitcast_fusion) | data formatting | bytes 8388608 | tf_op jit(solution)/shard_map/convert_element_type | solution.py:144
  143.4 7.0 %reshape.180 = bf16[2,128,64,64]{3,2,1,0:T(8,128)(2,1)} reshape(bf16[256,4096]{1,0:T(8,128)(2,1)} %copy-done.1) | data formatting | bytes 4194304 | tf_op jit(solution)/shard_map/reshape | solution.py:101
  150.8 6.6 %copy.82 = bf16[2,128,64,64]{1,3,2,0:T(8,128)(2,1)} copy(bf16[2,128,64,64]{3,2,1,0:T(8,128)(2,1)} %reshape.180) | data formatting | bytes 4194304 | tf_op jit(solution)/shard_map/reshape | solution.py:101
  157.7 107.7 %all-gather.4.cloned.1.call-done = f32[16,64,64,128]{3,2,1,0:T(8,128)} async-done(((f32[1,64,64,128]{3,2,1,0:T(8,128)}), f32[16,64,64,128]{3,2,1,0:T(8,128)}) %all-gather.4.cloned.1.call-update) | async-done | bytes 33554448 | tf_op jit(solution)/shard_map/all_gather | solution.py:21
  265.4 42.4 %while.14 = (s32[]{:T(128)}, f32[64,64,128]{2,1,0:T(8,128)S(1)}, s32[]{:T(128)}, f32[16,64]{1,0:T(8,128)}, f32[16,64,64,128]{3,2,1,0:T(8,128)}, /*index=5*/s32[]{:T(128)}, s32[]{:T(128)}) while((s32[]{:T(128)}, f32[64,64,128]{2,1,0:T(8,128)S(1)}, s32[]{:T(128)}, f32[16,64]{1,0:T(8,128)}, f32[16,64,64,128]{3,2,1,0:T(8,128)}, ...), condition=%wide.region_3.4_spmd.clone, body=%wide.region_2.3_spmd.clone.sunk | while | flops 2097156 | bytes 6292329 | solution.py:30
  266.1 2.1 fusion.61
  268.9 2.1 fusion.61
  271.7 2.1 fusion.61
  274.5 2.3 fusion.61
  277.5 2.1 fusion.61
  280.3 2.1 fusion.61
  283.1 2.1 fusion.61
  286.0 2.1 fusion.61
  288.8 2.1 fusion.61
  291.6 2.1 fusion.61
  294.3 2.1 fusion.61
  297.1 2.1 fusion.61
  299.2 0.7 exponential_bitcast_fusion.2
  299.9 2.3 fusion.61
  302.2 0.7 exponential_bitcast_fusion.2
  302.9 2.1 fusion.61
  305.7 2.1 fusion.61
  307.9 2.1 fusion.51
  310.0 0.7 fusion.17
  310.8 1.0 mul.315
  312.3 8.7 %multiply_reduce_fusion = (f32[2,128,64]{1,2,0:T(8,128)S(1)}, f32[2,128,64,64]{1,3,2,0:T(8,128)}) fusion(bf16[128,2,4096]{0,2,1:T(8,128)(2,1)} %all-to-all-done.4, bf16[2,128,64,64]{1,3,2,0:T(8,128)(2,1)S(1)} %copy-done.5, f32[64]{0:T(128)S(1)} %copy-done.32, f32[2,128,64,64]{1,3,2,0:T(8,128)S(1)} %bitcast.142, f32[2,128,64]{1,2,0:T(8,128)S(1)} %copy.89, ...), kind=kOutput, calls=%fused_computation.24 | convolution fusion | flops 292536320 | bytes 21250304 | tf_op jit(solution)/shard_map/khts,kshp->kthp/dot_general | solution.py:109
  321.0 9.2 %copy.103 = f32[2,128,64,64]{3,2,1,0:T(8,128)} copy(f32[2,128,64,64]{1,3,2,0:T(8,128)} %get-tuple-element.155) | data formatting | bytes 8388608 | tf_op jit(solution)/shard_map/reshape | solution.py:143
  330.2 8.0 %reshape.179 = f32[256,4096]{1,0:T(8,128)} reshape(f32[2,128,64,64]{3,2,1,0:T(8,128)} %copy.103) | data formatting | bytes 8388608 | tf_op jit(solution)/shard_map/reshape | solution.py:143
  339.1 3.9 copy.107
  343.1 1.8 multiply_convert_fusion.2
  344.9 97.2 %all-gather.6.cloned.1.call-done = bf16[4096,4096]{1,0:T(8,128)(2,1)} async-done(((bf16[4096,256]{1,0:T(8,128)(2,1)}), bf16[4096,4096]{1,0:T(8,128)(2,1)}) %all-gather.6.cloned.1.call-update) | async-done | bytes 33554448 | tf_op jit(solution)/shard_map/all_gather | solution.py:150
  442.1 16.6 %convolution_convert_fusion = bf16[256,4096]{1,0:T(8,128)(2,1)} fusion(bf16[256,4096]{1,0:T(8,128)(2,1)S(1)} %multiply_convert_fusion.2, bf16[4096,4096]{1,0:T(8,128)(2,1)} %all-gather.6.cloned.1.call-done), kind=kOutput, calls=%fused_computation.4 | convolution fusion | flops 8590983168 | bytes 37748736 | tf_op jit(solution)/shard_map/dot_general | solution.py:148
  458.8 30.8 %reduce-scatter.2.cloned.1.call-done = bf16[128,4096]{1,0:T(8,128)(2,1)} async-done(((bf16[256,4096]{1,0:T(8,128)(2,1)}), bf16[128,4096]{1,0:T(8,128)(2,1)}) %reduce-scatter.2.cloned.1.call-update) | async-done | bytes 1048592 | tf_op jit(solution)/shard_map/reduce_scatter | solution.py:153
  (127 shorter events, 19.5 us)
Async XLA Ops:
  6.5 10.6 %copy-start.7 = (bf16[128,1024]{1,0:T(8,128)(2,1)S(1)}, bf16[128,1024]{1,0:T(8,128)(2,1)}, u32[]{:S(2)}) copy-start(bf16[128,1024]{1,0:T(8,128)(2,1)} %param.18) | copy-start | bytes 786436
  6.5 11.4 %copy-start.8 = (bf16[128,1024]{1,0:T(8,128)(2,1)S(1)}, bf16[128,1024]{1,0:T(8,128)(2,1)}, u32[]{:S(2)}) copy-start(bf16[128,1024]{1,0:T(8,128)(2,1)} %param.19) | copy-start | bytes 786436
  6.5 15.7 %copy-start.15 = (f32[4,2,512]{2,1,0:T(2,128)S(1)}, f32[4,2,512]{2,1,0:T(2,128)}, u32[]{:S(2)}) copy-start(f32[4,2,512]{2,1,0:T(2,128)} %param.26) | copy-start | bytes 49156
  6.5 24.6 %copy-start.26 = (f32[2,512]{1,0:T(2,128)S(1)}, f32[2,512]{1,0:T(2,128)}, u32[]{:S(2)}) copy-start(f32[2,512]{1,0:T(2,128)} %param.27) | copy-start | bytes 12292
  8.1 10.7 %all-to-all-start.3 = ((bf16[128,2,64]{0,2,1:T(8,128)(2,1)}), bf16[128,2,64]{0,2,1:T(8,128)(2,1)S(1)}, u32[]{:S(2)}, u32[]{:S(2)}) async-start(bf16[128,2,64]{0,2,1:T(8,128)(2,1)} %bitcast.13), calls=%async_computation.3 | async-start | bytes 65536 | tf_op jit(solution)/shard_map/all_to_all | solution.py:81
  17.1 23.0 %copy-start.31 = (f32[64]{0:T(128)S(1)}, f32[64]{0:T(128)}, u32[]{:S(2)}) copy-start(f32[64]{0:T(128)} %param.22) | copy-start | bytes 772
  17.1 23.2 %copy-start.24 = (f32[64]{0:T(128)S(1)}, f32[64]{0:T(128)}, u32[]{:S(2)}) copy-start(f32[64]{0:T(128)} %param.21) | copy-start | bytes 772
  18.8 8.9 %all-to-all-start.1 = ((bf16[128,2,512]{0,2,1:T(8,128)(2,1)}), bf16[128,2,512]{0,2,1:T(8,128)(2,1)S(1)}, u32[]{:S(2)}, u32[]{:S(2)}) async-start(bf16[128,2,512]{0,2,1:T(8,128)(2,1)} %bitcast.4), calls=%async_computation.1 | async-start | bytes 524288 | tf_op jit(solution)/shard_map/all_to_all | solution.py:79
  27.7 8.6 %all-to-all-start.2 = ((bf16[128,2,512]{0,2,1:T(8,128)(2,1)}), bf16[128,2,512]{0,2,1:T(8,128)(2,1)S(1)}, u32[]{:S(2)}, u32[]{:S(2)}) async-start(bf16[128,2,512]{0,2,1:T(8,128)(2,1)} %bitcast.7), calls=%async_computation.2 | async-start | bytes 524288 | tf_op jit(solution)/shard_map/all_to_all | solution.py:80
  36.3 26.9 %all-to-all-start = ((bf16[128,2,4096]{0,2,1:T(8,128)(2,1)}), bf16[128,2,4096]{0,2,1:T(8,128)(2,1)S(1)}, u32[]{:S(2)}, u32[]{:S(2)}) async-start(bf16[128,2,4096]{0,2,1:T(8,128)(2,1)} %bitcast.1), calls=%async_computation | async-start | bytes 4194304 | tf_op jit(solution)/shard_map/all_to_all | solution.py:77
  40.1 225.3 %all-gather.4.cloned.1.call-start = ((), (), s32[]{:S(2)}) async-start(), calls=%async_computation.6 | async-start | bytes 35651584 | tf_op jit(solution)/shard_map/all_gather | solution.py:21
  63.2 1.3 copy-start.4
  67.5 6.2 %collective-permute-start = (bf16[3,5120]{1,0:T(4,128)(2,1)S(1)}, bf16[3,5120]{1,0:T(4,128)(2,1)S(1)}, u32[]{:S(2)}, u32[]{:S(2)}) collective-permute-start(bf16[3,5120]{1,0:T(4,128)(2,1)S(1)} %pad_maximum_fusion), channel_id=1, source_target_pairs={{0,2},{2,4},{4,6},{6,8},{8,10},{10,12},{12,14},{14,16},{16,18},{18... | collective-permute-start | bytes 92168 | tf_op jit(solution)/shard_map/ppermute | solution.py:16
  73.7 0.6 copy-start.14
  75.6 1.5 copy-start.10
  75.6 1.5 copy-start.11
  75.6 1.5 copy-start.12
  75.6 1.5 copy-start.13
  75.6 1.5 copy-start.17
  79.8 8.9 %copy-start.1 = (bf16[256,4096]{1,0:T(8,128)(2,1)}, bf16[256,4096]{1,0:T(8,128)(2,1)S(1)}, u32[]{:S(2)}) copy-start(bf16[256,4096]{1,0:T(8,128)(2,1)S(1)} %multiply_convert_fusion.4) | copy-start | bytes 6291460
  94.0 1.9 copy-start.28
  94.0 1.9 copy-start.30
  94.6 1.3 copy-start
  95.9 2.4 copy-start.6
  97.6 344.5 %all-gather.6.cloned.1.call-start = ((), (), s32[]{:S(2)}) async-start(), calls=%async_computation.7 | async-start | bytes 35651584 | tf_op jit(solution)/shard_map/all_gather | solution.py:150
  98.4 7.4 %copy-start.33 = (u32[32]{0:T(128)S(1)}, u32[32]{0:T(128)}, u32[]{:S(2)}) copy-start(u32[32]{0:T(128)} %constant.53) | copy-start | bytes 388
  98.4 9.3 %copy-start.29 = (f32[64]{0:T(128)S(1)}, f32[64]{0:T(128)}, u32[]{:S(2)}) copy-start(f32[64]{0:T(128)} %get-tuple-element.136) | copy-start | bytes 772
  98.4 34.6 %copy-start.25 = (f32[64]{0:T(128)S(1)}, f32[64]{0:T(128)}, u32[]{:S(2)}) copy-start(f32[64]{0:T(128)} %param.21) | copy-start | bytes 772
  100.9 33.0 %all-to-all-start.4 = ((bf16[128,2,4096]{0,2,1:T(8,128)(2,1)}), bf16[128,2,4096]{0,2,1:T(8,128)(2,1)}, u32[]{:S(2)}, u32[]{:S(2)}) async-start(bf16[128,2,4096]{0,2,1:T(8,128)(2,1)} %bitcast.43), calls=%async_computation.4 | async-start | bytes 4194304 | tf_op jit(solution)/shard_map/all_to_all | solution.py:78
  105.7 383.9 %reduce-scatter.2.cloned.1.call-start = ((), (), s32[]{:S(2)}) async-start(), calls=%async_computation.8 | async-start | bytes 3145728 | tf_op jit(solution)/shard_map/reduce_scatter | solution.py:153
  143.4 7.0 %copy-start.19 = (f32[1,1,512]{2,1,0:T(1,128)S(1)}, f32[1,1,512]{2,1,0:T(1,128)}, u32[]{:S(2)}) copy-start(f32[1,1,512]{2,1,0:T(1,128)} %get-tuple-element.144) | copy-start | bytes 6148
  143.4 7.0 %copy-start.20 = (f32[1,1,512]{2,1,0:T(1,128)S(1)}, f32[1,1,512]{2,1,0:T(1,128)}, u32[]{:S(2)}) copy-start(f32[1,1,512]{2,1,0:T(1,128)} %get-tuple-element.147) | copy-start | bytes 6148
  143.4 7.0 %copy-start.21 = (f32[1,1,512]{2,1,0:T(1,128)S(1)}, f32[1,1,512]{2,1,0:T(1,128)}, u32[]{:S(2)}) copy-start(f32[1,1,512]{2,1,0:T(1,128)} %get-tuple-element.148) | copy-start | bytes 6148
  143.4 7.0 %copy-start.22 = (f32[1,1,512]{2,1,0:T(1,128)S(1)}, f32[1,1,512]{2,1,0:T(1,128)}, u32[]{:S(2)}) copy-start(f32[1,1,512]{2,1,0:T(1,128)} %get-tuple-element.149) | copy-start | bytes 6148
  143.4 7.0 %copy-start.23 = (f32[1,512]{1,0:T(1,128)S(1)}, f32[1,512]{1,0:T(1,128)}, u32[]{:S(2)}) copy-start(f32[1,512]{1,0:T(1,128)} %get-tuple-element.152) | copy-start | bytes 6148
  265.4 42.5 %copy-start.27 = (f32[64]{0:T(128)S(1)}, f32[64]{0:T(128)}, u32[]{:S(2)}) copy-start(f32[64]{0:T(128)} %get-tuple-element.134) | copy-start | bytes 772
  310.7 1.6 copy-start.5
  310.8 1.6 copy-start.9
  310.8 1.6 copy-start.16
  310.8 1.6 copy-start.32
  338.5 4.6 copy-start.18
  339.1 4.0 copy-start.2
  339.1 4.0 copy-start.3
Sparse Core Ops, SparseCore 0:
  97.7 167.6 all-gather.3
  266.9 175.1 all-gather.5
  458.9 30.6 reduce-scatter.1
where the time goes:
time: 500 us; the launch traced here: 496 us
  waiting for transfers between devices  271 us (54%)
  local copies, waits for them, and re-layouts  85.9 us (17%)
  other arithmetic  52.8 us (11%)
  matrix products  27 us (5%)
  blocking collectives  24.4 us (5%)
  starting transfers between devices  20.8 us (4%)
  between operations  14.4 us (3%)
    all_gather x1, waiting for transfers between devices, prefix(): pieces = jax.tree.map(lambda part: lax.all_gather(part, axis), value)  108 us
    all_gather x1, waiting for transfers between devices, per_device(): lax.all_gather(out_weight, 'seq', axis=1, tiled=True)  97.2 us
    select_n x15, other arithmetic, lap(): jnp.where(position < mine, new, old)  31.8 us
    reduce_scatter x1, waiting for transfers between devices, per_device(): lax.psum_scatter(terms.astype(jnp.bfloat16), 'head', scatter_dimension=0,...  30.8 us
    unnamed x1, blocking collectives  24.4 us
    all_to_all x1, waiting for transfers between devices, per_device(): lax.all_to_all(x_proj, 'head', split_axis=1, concat_axis=0, tiled=True)  21 us
    unnamed x77, local copies, waits for them, and re-layouts  18.4 us
    reshape x2, local copies, waits for them, and re-layouts, per_device(): outputs = outputs.reshape(token_count, local_heads * HEAD_DIM)  17.2 us
  transfers between devices with their start and end apart: 9, of which 7 were waited for; matrix products, arithmetic and copies ran while one was open for 24% of the time, Pallas kernels for 0%

commit v1 on v0

--- a/solution.py
+++ b/solution.py
@@ -16,18 +16,22 @@
     return lax.ppermute(array, axis, pairs)
 
 
-def prefix(value, axis, join, neutral):
+def carry_in(log_total, final_state, axis):
     count, mine = (lax.axis_size(axis), lax.axis_index(axis))
-    pieces = jax.tree.map(lambda part: lax.all_gather(part, axis), value)
-    total = jax.tree.map(
-        lambda part, zero: jnp.full_like(part, 0) + jnp.asarray(zero, part.dtype), value, neutral
-    )
-
-    def lap(position, total):
-        longer = join(total, jax.tree.map(lambda part: part[position], pieces))
-        return jax.tree.map(lambda new, old: jnp.where(position < mine, new, old), longer, total)
-
-    return lax.fori_loop(0, count - 1, lap, total)
+    width = final_state.shape[-1]
+    flat = final_state.reshape(count, -1, width).astype(jnp.bfloat16)
+    rows = flat.shape[1]
+    pieces = lax.all_to_all(flat, axis, split_axis=0, concat_axis=0)
+    logs = lax.all_gather(log_total, axis)
+    by_row = jnp.repeat(logs, final_state.shape[1], axis=1)
+    decays = jnp.exp(lax.dynamic_slice_in_dim(by_row, mine * rows, rows, axis=1))
+    running = jnp.zeros((rows, width), jnp.float32)
+    starts = []
+    for position in range(count):
+        starts.append(running.astype(jnp.bfloat16))
+        running = decays[position][:, None] * running + pieces[position].astype(jnp.float32)
+    back = lax.all_to_all(jnp.stack(starts), axis, split_axis=0, concat_axis=0)
+    return back.reshape(final_state.shape).astype(jnp.float32)
 
 
 def depthwise(current, previous, weight, bias_row):
@@ -51,10 +55,6 @@
     head_count = cumulative.shape[2]
     grouped = scaled.reshape(block_count, -1, per_group, length, length) * scores[:, :, None]
     return grouped.reshape(block_count, head_count, length, length).astype(jnp.bfloat16)
-
-
-def combine_states(earlier, later):
-    return (earlier[0] + later[0], jnp.exp(later[0])[:, None, None] * earlier[1] + later[1])
 
 
 def per_device(
@@ -121,13 +121,7 @@
     for block_idx in range(blocks):
         final_state = jnp.exp(totals[block_idx])[:, None, None] * final_state + pieces[block_idx]
     log_total = jnp.sum(totals, axis=0)
-    carried = prefix(
-        (log_total, final_state),
-        "seq",
-        combine_states,
-        (jnp.zeros_like(log_total), jnp.zeros_like(final_state)),
-    )
-    running = carried[1]
+    running = carry_in(log_total, final_state, "seq")
     start_list = []
     for block_idx in range(blocks):
         start_list.append(running.astype(jnp.bfloat16))

time: 500 us -> 324 us (0.65)
  waiting for transfers between devices: 271 us -> 66.9 us
  blocking collectives: 24.4 us -> 47 us
  starting transfers between devices: 20.8 us -> 37.5 us
  local copies, waits for them, and re-layouts: 85.9 us -> 77.6 us
  other arithmetic: 52.8 us -> 47.6 us
    all_gather x1 -> x0, waiting for transfers between devices: 108 us -> none  [prefix(): pieces = jax.tree.map(lambda part: lax.all_gather(part, axis), value)]
    all_gather x1, waiting for transfers between devices: 97.2 us -> 0.02 us  [per_device(): lax.all_gather(out_weight, 'seq', axis=1, tiled=True)]
    select_n x15 -> x0, other arithmetic: 31.8 us -> none  [lap(): jnp.where(position < mine, new, old)]
    unnamed x1 -> x14, other arithmetic: 0.01 us -> 23.1 us
    unnamed x1, blocking collectives: 24.4 us -> 47 us
    all_to_all x0 -> x2, starting transfers between devices: none -> 16.7 us  [the longest x1 11.3 us: carry_in(): back = lax.all_to_all(jnp.stack(starts), axis, split_axis=0, concat_axis=0)]
    exp x15 -> x1, local copies, waits for them, and re-layouts: 10.3 us -> 0.72 us  [carry_in(): jnp.exp(lax.dynamic_slice_in_dim(by_row, mine * rows, rows, axis=1))]
    unnamed x77 -> x74, local copies, waits for them, and re-layouts: 18.4 us -> 19.1 us
  transfers between devices with their start and end apart: 9 -> 10, of which waited for: 7 -> 8; matrix products, arithmetic and copies ran while one was open for 24% -> 42% of each run, Pallas kernels for 0% -> 0%
where the time goes in v1:
time: 324 us; the launch traced here: 320 us
  local copies, waits for them, and re-layouts  77.6 us (24%)
  waiting for transfers between devices  66.9 us (21%)
  other arithmetic  47.6 us (15%)
  blocking collectives  47 us (15%)
  starting transfers between devices  37.5 us (12%)
  matrix products  28.3 us (9%)
  between operations  14.7 us (5%)
    unnamed x1, blocking collectives  47 us
    reduce_scatter x1, waiting for transfers between devices, per_device(): lax.psum_scatter(terms.astype(jnp.bfloat16), 'head', scatter_dimension=0,...  33.3 us
    unnamed x14, other arithmetic  23.1 us
    all_to_all x1, waiting for transfers between devices, per_device(): lax.all_to_all(x_proj, 'head', split_axis=1, concat_axis=0, tiled=True)  20.4 us
    unnamed x74, local copies, waits for them, and re-layouts  19.1 us
    reshape x2, local copies, waits for them, and re-layouts, per_device(): outputs = outputs.reshape(token_count, local_heads * HEAD_DIM)  17.1 us
    dot_general x1, matrix products, per_device(): jnp.dot(normed, lax.all_gather(out_weight, 'seq', axis=1, tiled=True), pr...  16.6 us
    reshape x2, local copies, waits for them, and re-layouts, per_device(): x_blocks = x_conv.reshape(blocks, SPAN, local_heads, HEAD_DIM)  11.5 us
  transfers between devices with their start and end apart: 10, of which 8 were waited for; matrix products, arithmetic and copies ran while one was open for 42% of the time, Pallas kernels for 0%

profile of v1, /device:TPU:8, one launch (start us, length us, event | category | flops | bytes accessed | tf_op | source)
XLA Modules:
  0.0 319.7 jit_solution(6257656156289535702)
XLA Ops:
  7.3 1.5 copy.75
  8.7 3.3 %all-to-all-start.3 = ((bf16[128,2,64]{0,2,1:T(8,128)(2,1)}), bf16[128,2,64]{0,2,1:T(8,128)(2,1)S(1)}, u32[]{:S(2)}, u32[]{:S(2)}) async-start(bf16[128,2,64]{0,2,1:T(8,128)(2,1)} %bitcast.13), calls=%async_computation.3 | async-start | bytes 65536 | tf_op jit(solution)/shard_map/all_to_all | solution.py:81
  12.0 1.8 copy.70
  13.8 2.2 all-to-all-done.3
  15.9 3.4 %all-to-all-start.1 = ((bf16[128,2,512]{0,2,1:T(8,128)(2,1)}), bf16[128,2,512]{0,2,1:T(8,128)(2,1)S(1)}, u32[]{:S(2)}, u32[]{:S(2)}) async-start(bf16[128,2,512]{0,2,1:T(8,128)(2,1)} %bitcast.4), calls=%async_computation.1 | async-start | bytes 524288 | tf_op jit(solution)/shard_map/all_to_all | solution.py:79
  19.4 1.7 fusion.68
  21.1 2.5 copy.68
  23.6 0.8 copy.72
  24.5 3.4 %all-to-all-start.2 = ((bf16[128,2,512]{0,2,1:T(8,128)(2,1)}), bf16[128,2,512]{0,2,1:T(8,128)(2,1)S(1)}, u32[]{:S(2)}, u32[]{:S(2)}) async-start(bf16[128,2,512]{0,2,1:T(8,128)(2,1)} %bitcast.7), calls=%async_computation.2 | async-start | bytes 524288 | tf_op jit(solution)/shard_map/all_to_all | solution.py:80
  28.6 4.5 %all-to-all-done.2 = bf16[128,2,512]{0,2,1:T(8,128)(2,1)S(1)} async-done(((bf16[128,2,512]{0,2,1:T(8,128)(2,1)}), bf16[128,2,512]{0,2,1:T(8,128)(2,1)S(1)}, u32[]{:S(2)}, u32[]{:S(2)}) %all-to-all-start.2) | async-done | bytes 262176 | tf_op jit(solution)/shard_map/all_to_all | solution.py:80
  33.2 3.8 %all-to-all-start = ((bf16[128,2,4096]{0,2,1:T(8,128)(2,1)}), bf16[128,2,4096]{0,2,1:T(8,128)(2,1)S(1)}, u32[]{:S(2)}, u32[]{:S(2)}) async-start(bf16[128,2,4096]{0,2,1:T(8,128)(2,1)} %bitcast.1), calls=%async_computation | async-start | bytes 4194304 | tf_op jit(solution)/shard_map/all_to_all | solution.py:77
  38.6 0.8 fusion.66
  39.7 20.4 %all-to-all-done = bf16[128,2,4096]{0,2,1:T(8,128)(2,1)S(1)} async-done(((bf16[128,2,4096]{0,2,1:T(8,128)(2,1)}), bf16[128,2,4096]{0,2,1:T(8,128)(2,1)S(1)}, u32[]{:S(2)}, u32[]{:S(2)}) %all-to-all-start) | async-done | bytes 2097184 | tf_op jit(solution)/shard_map/all_to_all | solution.py:77
  60.1 1.3 copy-done.3
  61.4 2.9 copy.69
  64.4 1.9 collective-permute-start
  67.6 4.0 %collective-permute-done = bf16[3,5120]{1,0:T(4,128)(2,1)S(1)} collective-permute-done((bf16[3,5120]{1,0:T(4,128)(2,1)S(1)}, bf16[3,5120]{1,0:T(4,128)(2,1)S(1)}, u32[]{:S(2)}, u32[]{:S(2)}) %collective-permute-start) | collective-permute-done | bytes 30752 | tf_op jit(solution)/shard_map/ppermute | solution.py:16
  71.8 1.1 multiply_convert_fusion.7
  73.7 2.7 multiply_convert_fusion.4
  76.4 2.9 copy.83
  79.3 5.8 %reshape.881 = f32[2,128,4,16,64]{1,0,4,3,2:T(2,128)} reshape(f32[256,4096]{0,1:T(8,128)} %copy.83) | data formatting | bytes 8388608 | tf_op jit(solution)/shard_map/convert_element_type | solution.py:113
  85.2 4.5 %multiply_convert_fusion.3 = bf16[2,128,4,16,64]{1,0,4,3,2:T(2,128)(2,1)S(1)} fusion(f32[2,128,4,16,64]{1,0,4,3,2:T(2,128)} %reshape.881, f32[2,128,4,16]{1,0,3,2:T(2,128)S(1)} %copy.85), kind=kLoop, calls=%fused_computation.22 | loop fusion | flops 2097152 | bytes 6356992 | tf_op jit(solution)/shard_map/convert_element_type | solution.py:113
  91.0 1.6 copy-done
  92.6 2.5 add_convert_fusion.1
  95.1 5.3 %all-to-all-start.4 = ((bf16[16,256,128]{2,1,0:T(8,128)(2,1)}), bf16[16,256,128]{2,1,0:T(8,128)(2,1)}, u32[]{:S(2)}, u32[]{:S(2)}) async-start(bf16[16,256,128]{2,1,0:T(8,128)(2,1)} %add_convert_fusion.1), calls=%async_computation.4 | async-start | bytes 2097152 | tf_op jit(solution)/shard_map/all_to_all | solution.py:24
  100.5 4.1 %copy.92 = bf16[128,8192]{0,1:T(8,128)(2,1)} copy(bf16[128,8192]{1,0:T(8,128)(2,1)} %param.15) | data formatting | bytes 4194304 | tf_op args[1]
  106.6 47.0 %all-reduce = f32[1024]{0:T(1024)S(1)} all-reduce(f32[1024]{0:T(1024)S(1)} %dynamic-update-slice), channel_id=2, replica_groups=mesh['seq'=16,'head'=2] {'seq'}, use_global_device_ids=true, to_apply=%add | all-reduce | flops 1024 | bytes 8192
  154.3 0.9 broadcast_in_dim.46
  155.2 0.9 reshape.878
  156.1 0.7 dynamic-slice_exponential_fusion
  156.9 5.0 %all-to-all-start.6 = ((bf16[128,2,4096]{0,2,1:T(8,128)(2,1)}), bf16[128,2,4096]{0,2,1:T(8,128)(2,1)}, u32[]{:S(2)}, u32[]{:S(2)}) async-start(bf16[128,2,4096]{0,2,1:T(8,128)(2,1)} %bitcast.131), calls=%async_computation.6 | async-start | bytes 4194304 | tf_op jit(solution)/shard_map/all_to_all | solution.py:78
  161.9 1.7 fusion.59
  163.6 1.6 fusion.58
  165.3 1.7 convert_dynamic-update-slice_fusion.5
  167.0 1.8 fusion.57
  168.8 1.8 convert_dynamic-update-slice_fusion.4
  170.6 1.6 fusion.56
  172.2 1.6 convert_dynamic-update-slice_fusion.3
  173.8 1.6 fusion.55
  175.4 1.6 convert_dynamic-update-slice_fusion.2
  177.0 1.6 fusion.54
  178.6 1.6 convert_dynamic-update-slice_fusion.1
  180.2 1.6 fusion.53
  181.8 1.6 convert_dynamic-update-slice_fusion
  183.4 1.6 fusion.52
  185.0 1.6 fusion.60
  186.7 0.7 all-to-all-done.6
  187.4 11.3 %all-to-all-start.5 = ((bf16[16,256,128]{2,1,0:T(8,128)(2,1)}), bf16[16,256,128]{2,1,0:T(8,128)(2,1)}, u32[]{:S(2)}, u32[]{:S(2)}) async-start(bf16[16,256,128]{2,1,0:T(8,128)(2,1)} %fusion.60), calls=%async_computation.5 | async-start | bytes 2097152 | tf_op jit(solution)/shard_map/all_to_all | solution.py:33
  199.4 1.3 exp.84
  202.3 3.9 %convert_bitcast_fusion = f32[2,128,4096]{1,2,0:T(8,128)} fusion(bf16[128,2,4096]{0,2,1:T(8,128)(2,1)} %all-to-all-done.6), kind=kLoop, calls=%fused_computation.38 | loop fusion | flops 1048576 | bytes 6291456 | tf_op jit(solution)/shard_map/convert_element_type | solution.py:138
  206.2 5.6 %copy.93 = f32[2,128,4096]{2,1,0:T(8,128)} copy(f32[2,128,4096]{1,2,0:T(8,128)} %convert_bitcast_fusion) | data formatting | bytes 8388608 | tf_op jit(solution)/shard_map/convert_element_type | solution.py:138
  211.9 5.6 %reshape.893 = bf16[2,128,64,64]{3,2,1,0:T(8,128)(2,1)} reshape(bf16[256,4096]{1,0:T(8,128)(2,1)S(1)} %multiply_convert_fusion.4) | data formatting | bytes 4194304 | tf_op jit(solution)/shard_map/reshape | solution.py:101
  217.9 5.9 %copy.82 = bf16[2,128,64,64]{1,3,2,0:T(8,128)(2,1)S(1)} copy(bf16[2,128,64,64]{3,2,1,0:T(8,128)(2,1)} %reshape.893) | data formatting | bytes 4194304 | tf_op jit(solution)/shard_map/reshape | solution.py:101
  224.2 0.9 all-to-all-done.5
  225.0 2.3 add_convert_fusion
  227.3 1.9 fusion.16
  229.3 1.0 mul.539
  230.4 8.7 %multiply_reduce_fusion = (f32[2,128,64]{1,2,0:T(8,128)S(1)}, f32[2,128,64,64]{1,3,2,0:T(8,128)}) fusion(bf16[128,2,4096]{0,2,1:T(8,128)(2,1)} %all-to-all-done.6, bf16[2,128,64,64]{1,3,2,0:T(8,128)(2,1)S(1)} %copy.82, f32[64]{0:T(128)S(1)} %copy-done.30, f32[2,128,64,64]{1,3,2,0:T(8,128)S(1)} %bitcast.135, f32[2,128,64]{1,2,0:T(8,128)S(1)} %copy-done.9, ...), kind=kOutput, calls=%fused_computation.21 | convolution fusion | flops 292536320 | bytes 21250304 | tf_op jit(solution)/shard_map/khts,kshp->kthp/dot_general | solution.py:109
  239.0 9.2 %copy.103 = f32[2,128,64,64]{3,2,1,0:T(8,128)} copy(f32[2,128,64,64]{1,3,2,0:T(8,128)} %get-tuple-element.56) | data formatting | bytes 8388608 | tf_op jit(solution)/shard_map/reshape | solution.py:137
  248.2 7.9 %reshape.892 = f32[256,4096]{1,0:T(8,128)} reshape(f32[2,128,64,64]{3,2,1,0:T(8,128)} %copy.103) | data formatting | bytes 8388608 | tf_op jit(solution)/shard_map/reshape | solution.py:137
  257.1 3.9 %copy.107 = f32[32,8,4,1024]{3,1,2,0:T(8,128)S(1)} copy(f32[32,8,4,1024]{3,2,1,0:T(4,128)S(1)} %bitcast.126) | data formatting | bytes 8388608
  261.0 1.8 multiply_convert_fusion.2
  262.9 16.6 %convolution_convert_fusion = bf16[256,4096]{1,0:T(8,128)(2,1)} fusion(bf16[256,4096]{1,0:T(8,128)(2,1)S(1)} %multiply_convert_fusion.2, bf16[4096,4096]{1,0:T(8,128)(2,1)} %all-gather.3.cloned.1.call-done), kind=kOutput, calls=%fused_computation.1 | convolution fusion | flops 8590983168 | bytes 37748736 | tf_op jit(solution)/shard_map/dot_general | solution.py:142
  279.6 33.3 %reduce-scatter.2.cloned.1.call-done = bf16[128,4096]{1,0:T(8,128)(2,1)} async-done(((bf16[256,4096]{1,0:T(8,128)(2,1)}), bf16[128,4096]{1,0:T(8,128)(2,1)}) %reduce-scatter.2.cloned.1.call-update) | async-done | bytes 1048592 | tf_op jit(solution)/shard_map/reduce_scatter | solution.py:147
  (118 shorter events, 12.8 us)
Async XLA Ops:
  6.5 14.5 %copy-start.4 = (bf16[128,8192]{1,0:T(8,128)(2,1)S(1)}, bf16[128,8192]{1,0:T(8,128)(2,1)}, u32[]{:S(2)}) copy-start(bf16[128,8192]{1,0:T(8,128)(2,1)} %param.14) | copy-start | bytes 6291460
  6.5 17.1 %copy-start.8 = (bf16[128,1024]{1,0:T(8,128)(2,1)S(1)}, bf16[128,1024]{1,0:T(8,128)(2,1)}, u32[]{:S(2)}) copy-start(bf16[128,1024]{1,0:T(8,128)(2,1)} %param.17) | copy-start | bytes 786436
  6.5 21.5 %copy-start.27 = (f32[2,512]{1,0:T(2,128)S(1)}, f32[2,512]{1,0:T(2,128)}, u32[]{:S(2)}) copy-start(f32[2,512]{1,0:T(2,128)} %param.25) | copy-start | bytes 12292
  6.5 256.3 %all-gather.3.cloned.1.call-start = ((), (), s32[]{:S(2)}) async-start(), calls=%async_computation.8 | async-start | bytes 35651584 | tf_op jit(solution)/shard_map/all_gather | solution.py:144
  8.7 7.2 %all-to-all-start.3 = ((bf16[128,2,64]{0,2,1:T(8,128)(2,1)}), bf16[128,2,64]{0,2,1:T(8,128)(2,1)S(1)}, u32[]{:S(2)}, u32[]{:S(2)}) async-start(bf16[128,2,64]{0,2,1:T(8,128)(2,1)} %bitcast.13), calls=%async_computation.3 | async-start | bytes 65536 | tf_op jit(solution)/shard_map/all_to_all | solution.py:81
  15.9 8.6 %all-to-all-start.1 = ((bf16[128,2,512]{0,2,1:T(8,128)(2,1)}), bf16[128,2,512]{0,2,1:T(8,128)(2,1)S(1)}, u32[]{:S(2)}, u32[]{:S(2)}) async-start(bf16[128,2,512]{0,2,1:T(8,128)(2,1)} %bitcast.4), calls=%async_computation.1 | async-start | bytes 524288 | tf_op jit(solution)/shard_map/all_to_all | solution.py:79
  21.1 15.9 %copy-start.29 = (f32[64]{0:T(128)S(1)}, f32[64]{0:T(128)}, u32[]{:S(2)}) copy-start(f32[64]{0:T(128)} %param.20) | copy-start | bytes 772
  21.1 15.9 %copy-start.15 = (f32[4,2,512]{2,1,0:T(2,128)S(1)}, f32[4,2,512]{2,1,0:T(2,128)}, u32[]{:S(2)}) copy-start(f32[4,2,512]{2,1,0:T(2,128)} %param.24) | copy-start | bytes 49156
  21.1 16.6 %copy-start.25 = (f32[64]{0:T(128)S(1)}, f32[64]{0:T(128)}, u32[]{:S(2)}) copy-start(f32[64]{0:T(128)} %param.19) | copy-start | bytes 772
  24.5 8.6 %all-to-all-start.2 = ((bf16[128,2,512]{0,2,1:T(8,128)(2,1)}), bf16[128,2,512]{0,2,1:T(8,128)(2,1)S(1)}, u32[]{:S(2)}, u32[]{:S(2)}) async-start(bf16[128,2,512]{0,2,1:T(8,128)(2,1)} %bitcast.7), calls=%async_computation.2 | async-start | bytes 524288 | tf_op jit(solution)/shard_map/all_to_all | solution.py:80
  33.2 26.9 %all-to-all-start = ((bf16[128,2,4096]{0,2,1:T(8,128)(2,1)}), bf16[128,2,4096]{0,2,1:T(8,128)(2,1)S(1)}, u32[]{:S(2)}, u32[]{:S(2)}) async-start(bf16[128,2,4096]{0,2,1:T(8,128)(2,1)} %bitcast.1), calls=%async_computation | async-start | bytes 4194304 | tf_op jit(solution)/shard_map/all_to_all | solution.py:77
  37.7 33.9 %copy-start.5 = (bf16[128,2,64]{2,0,1:T(8,128)(2,1)}, bf16[128,2,64]{2,0,1:T(8,128)(2,1)S(1)}, u32[]{:S(2)}) copy-start(bf16[128,2,64]{2,0,1:T(8,128)(2,1)S(1)} %copy.76) | copy-start | bytes 98308
  60.1 1.3 copy-start.3
  64.4 7.2 %collective-permute-start = (bf16[3,5120]{1,0:T(4,128)(2,1)S(1)}, bf16[3,5120]{1,0:T(4,128)(2,1)S(1)}, u32[]{:S(2)}, u32[]{:S(2)}) collective-permute-start(bf16[3,5120]{1,0:T(4,128)(2,1)S(1)} %pad_maximum_fusion), channel_id=1, source_target_pairs={{0,2},{2,4},{4,6},{6,8},{8,10},{10,12},{12,14},{14,16},{16,18},{18... | collective-permute-start | bytes 92168 | tf_op jit(solution)/shard_map/ppermute | solution.py:16
  71.8 1.8 copy-start.11
  71.8 1.8 copy-start.12
  71.8 1.8 copy-start.13
  71.8 1.8 copy-start.14
  71.8 1.8 copy-start.17
  90.4 2.2 copy-start
  95.1 9.5 %copy-start.31 = (u32[32]{0:T(128)S(1)}, u32[32]{0:T(128)}, u32[]{:S(2)}) copy-start(u32[32]{0:T(128)} %constant.38) | copy-start | bytes 388
  95.1 11.3 %copy-start.28 = (f32[64]{0:T(128)S(1)}, f32[64]{0:T(128)}, u32[]{:S(2)}) copy-start(f32[64]{0:T(128)} %get-tuple-element.23) | copy-start | bytes 772
  95.1 61.7 %all-to-all-start.4 = ((bf16[16,256,128]{2,1,0:T(8,128)(2,1)}), bf16[16,256,128]{2,1,0:T(8,128)(2,1)}, u32[]{:S(2)}, u32[]{:S(2)}) async-start(bf16[16,256,128]{2,1,0:T(8,128)(2,1)} %add_convert_fusion.1), calls=%async_computation.4 | async-start | bytes 2097152 | tf_op jit(solution)/shard_map/all_to_all | solution.py:24
  156.9 30.6 %all-to-all-start.6 = ((bf16[128,2,4096]{0,2,1:T(8,128)(2,1)}), bf16[128,2,4096]{0,2,1:T(8,128)(2,1)}, u32[]{:S(2)}, u32[]{:S(2)}) async-start(bf16[128,2,4096]{0,2,1:T(8,128)(2,1)} %bitcast.131), calls=%async_computation.6 | async-start | bytes 4194304 | tf_op jit(solution)/shard_map/all_to_all | solution.py:78
  161.9 38.9 %copy-start.7 = (f32[2,128,64]{2,1,0:T(8,128)S(1)}, f32[2,128,64]{2,1,0:T(8,128)}, u32[]{:S(2)}) copy-start(f32[2,128,64]{2,1,0:T(8,128)} %get-tuple-element.20) | copy-start | bytes 196612
  161.9 40.3 %copy-start.6 = (bf16[128,2,64]{2,0,1:T(8,128)(2,1)S(1)}, bf16[128,2,64]{2,0,1:T(8,128)(2,1)}, u32[]{:S(2)}) copy-start(bf16[128,2,64]{2,0,1:T(8,128)(2,1)} %copy-done.5) | copy-start | bytes 98308
  161.9 40.3 %copy-start.26 = (f32[64]{0:T(128)S(1)}, f32[64]{0:T(128)}, u32[]{:S(2)}) copy-start(f32[64]{0:T(128)} %param.19) | copy-start | bytes 772
  187.4 37.6 %all-to-all-start.5 = ((bf16[16,256,128]{2,1,0:T(8,128)(2,1)}), bf16[16,256,128]{2,1,0:T(8,128)(2,1)}, u32[]{:S(2)}, u32[]{:S(2)}) async-start(bf16[16,256,128]{2,1,0:T(8,128)(2,1)} %fusion.60), calls=%async_computation.5 | async-start | bytes 2097152 | tf_op jit(solution)/shard_map/all_to_all | solution.py:33
  198.8 114.1 %reduce-scatter.2.cloned.1.call-start = ((), (), s32[]{:S(2)}) async-start(), calls=%async_computation.9 | async-start | bytes 3145728 | tf_op jit(solution)/shard_map/reduce_scatter | solution.py:147
  211.8 5.6 %copy-start.20 = (f32[1,1,512]{2,1,0:T(1,128)S(1)}, f32[1,1,512]{2,1,0:T(1,128)}, u32[]{:S(2)}) copy-start(f32[1,1,512]{2,1,0:T(1,128)} %get-tuple-element.30) | copy-start | bytes 6148
  211.9 5.6 %copy-start.21 = (f32[1,1,512]{2,1,0:T(1,128)S(1)}, f32[1,1,512]{2,1,0:T(1,128)}, u32[]{:S(2)}) copy-start(f32[1,1,512]{2,1,0:T(1,128)} %get-tuple-element.33) | copy-start | bytes 6148
  211.9 5.6 %copy-start.22 = (f32[1,1,512]{2,1,0:T(1,128)S(1)}, f32[1,1,512]{2,1,0:T(1,128)}, u32[]{:S(2)}) copy-start(f32[1,1,512]{2,1,0:T(1,128)} %get-tuple-element.34) | copy-start | bytes 6148
  211.9 5.6 %copy-start.23 = (f32[1,1,512]{2,1,0:T(1,128)S(1)}, f32[1,1,512]{2,1,0:T(1,128)}, u32[]{:S(2)}) copy-start(f32[1,1,512]{2,1,0:T(1,128)} %get-tuple-element.35) | copy-start | bytes 6148
  211.9 5.6 %copy-start.24 = (f32[1,512]{1,0:T(1,128)S(1)}, f32[1,512]{1,0:T(1,128)}, u32[]{:S(2)}) copy-start(f32[1,512]{1,0:T(1,128)} %get-tuple-element.53) | copy-start | bytes 6148
  217.8 7.2 %copy-start.19 = (f32[4,16]{1,0:T(4,128)S(1)}, f32[4,16]{1,0:T(4,128)}, u32[]{:S(2)}) copy-start(f32[4,16]{1,0:T(4,128)} %exp.84) | copy-start | bytes 772
  229.2 1.1 copy-start.9
  229.2 1.1 copy-start.10
  229.3 1.1 copy-start.16
  229.3 1.1 copy-start.30
  256.4 4.6 %copy-start.18 = (f32[4096]{0:T(1024)S(1)}, f32[4096]{0:T(1024)}, u32[]{:S(2)}) copy-start(f32[4096]{0:T(1024)} %param.26) | copy-start | bytes 49156
  257.1 4.0 %copy-start.1 = (f32[256,4096]{1,0:T(8,128)S(1)}, f32[256,4096]{1,0:T(8,128)}, u32[]{:S(2)}) copy-start(f32[256,4096]{1,0:T(8,128)} %reshape.892) | copy-start | bytes 12582916
  257.1 4.0 %copy-start.2 = (f32[2,128,4096]{2,1,0:T(8,128)S(1)}, f32[2,128,4096]{2,1,0:T(8,128)}, u32[]{:S(2)}) copy-start(f32[2,128,4096]{2,1,0:T(8,128)} %copy.93) | copy-start | bytes 12582916
Sparse Core Ops, SparseCore 0:
  8.8 212.9 all-gather.2
  279.7 33.1 reduce-scatter.1

commit v2 on v1

v2 whole, which is shorter than its diff:
```python
import functools

import jax
import jax.numpy as jnp
from jax import lax
from jax.experimental import pallas as pl
from jax.experimental.pallas import tpu as pltpu
from jax.sharding import PartitionSpec as P

HEAD_DIM = 64
STATE = 128
GROUPS = 8
SPAN = 128
DI = 8192
HALO = 16
NT = (((1,), (1,)), ((), ()))


def entry_kernel(count, heads, *refs):
    x_in, z_in, b_in, c_in, dt_in = refs[:5]
    x_out, z_out, b_out, c_out, dt_out, x_halo, b_halo, c_halo = refs[5:13]
    send_sems, recv_sems, local_sems, halo_send, halo_recv = refs[13:]
    seq = lax.axis_index("seq")
    head = lax.axis_index("head")
    rows = x_in.shape[0]
    barrier = pltpu.get_barrier_semaphore()
    last_head = head == heads - 1
    gives_halo = jnp.logical_and(last_head, seq < count - 1)
    takes_halo = seq > 0
    for step in range(1, heads):
        peer = lax.rem(head + step, heads)
        pl.semaphore_signal(
            barrier, inc=1, device_id=(seq, peer), device_id_type=pl.DeviceIdType.MESH
        )

    @pl.when(takes_halo)
    def _():
        pl.semaphore_signal(
            barrier,
            inc=1,
            device_id=(seq - 1, heads - 1),
            device_id_type=pl.DeviceIdType.MESH,
        )

    pl.semaphore_wait(barrier, heads - 1 + jnp.where(gives_halo, heads, 0))

    def columns(ref, width, which):
        return ref.at[:, pl.ds(pl.multiple_of(which * width, 128), width)]

    mine = pl.ds(pl.multiple_of(head * rows, 16), rows)
    plan = (
        (b_in, b_out, True),
        (c_in, c_out, True),
        (dt_in, dt_out, False),
        (x_in, x_out, True),
        (z_in, z_out, True),
    )
    halos = ((x_in, x_halo), (b_in, b_halo), (c_in, c_halo))

    def halo_copy(index, peer):
        source, target = halos[index]
        width = target.shape[1]
        return pltpu.make_async_remote_copy(
            src_ref=source.at[pl.ds(rows - HALO, HALO), pl.ds(peer * width, width)],
            dst_ref=target,
            send_sem=halo_send.at[index, peer],
            recv_sem=halo_recv.at[index],
            device_id=(seq + 1, peer),
            device_id_type=pl.DeviceIdType.MESH,
        )

    @pl.when(gives_halo)
    def _():
        for index in range(len(halos)):
            for peer in range(heads):
                halo_copy(index, peer).start()

    copies = []
    for step in range(1, heads):
        peer = lax.rem(head + step, heads)
        for index, (source, target, split) in enumerate(plan):
            view = columns(source, target.shape[1], peer) if split else source
            copy = pltpu.make_async_remote_copy(
                src_ref=view,
                dst_ref=target.at[mine],
                send_sem=send_sems.at[index, step],
                recv_sem=recv_sems.at[index, step],
                device_id=(seq, peer),
                device_id_type=pl.DeviceIdType.MESH,
            )
            copy.start()
            copies.append(copy)
    for index, (source, target, split) in enumerate(plan):
        view = columns(source, target.shape[1], head) if split else source
        copy = pltpu.make_async_copy(view, target.at[mine], local_sems.at[index])
        copy.start()
        copies.append(copy)

    @pl.when(jnp.logical_not(takes_halo))
    def _():
        for _, target in halos:
            target[...] = jnp.zeros_like(target)

    @pl.when(takes_halo)
    def _():
        for index, (source, target) in enumerate(halos):
            pltpu.make_async_remote_copy(
                src_ref=source.at[pl.ds(rows - HALO, HALO), pl.ds(0, target.shape[1])],
                dst_ref=target,
                send_sem=halo_send.at[index, 0],
                recv_sem=halo_recv.at[index],
                device_id=(seq, head),
                device_id_type=pl.DeviceIdType.MESH,
            ).wait_recv()

    @pl.when(gives_halo)
    def _():
        for index in range(len(halos)):
            for peer in range(heads):
                halo_copy(index, peer).wait_send()

    for copy in copies:
        copy.wait()


def entry_exchange(x_proj, z_proj, b_proj, c_proj, dt_raw):
    count = lax.axis_size("seq")
    heads = lax.axis_size("head")
    rows = x_proj.shape[0] * heads
    x_cols = x_proj.shape[1] // heads
    bc_cols = b_proj.shape[1] // heads
    dtype = x_proj.dtype
    shapes = [
        (rows, x_cols),
        (rows, x_cols),
        (rows, bc_cols),
        (rows, bc_cols),
        (rows, dt_raw.shape[1]),
        (HALO, x_cols),
        (HALO, bc_cols),
        (HALO, bc_cols),
    ]
    return pl.pallas_call(
        functools.partial(entry_kernel, count, heads),
        out_shape=[jax.ShapeDtypeStruct(shape, dtype) for shape in shapes],
        in_specs=[pl.BlockSpec(memory_space=pl.ANY)] * 5,
        out_specs=[pl.BlockSpec(memory_space=pl.ANY)] * 5
        + [pl.BlockSpec(memory_space=pltpu.VMEM)] * 3,
        scratch_shapes=[
            pltpu.SemaphoreType.DMA((5, heads)),
            pltpu.SemaphoreType.DMA((5, heads)),
            pltpu.SemaphoreType.DMA((5,)),
            pltpu.SemaphoreType.DMA((3, heads)),
            pltpu.SemaphoreType.DMA((3,)),
        ],
        compiler_params=pltpu.CompilerParams(collective_id=0, has_side_effects=True),
        name="entry_exchange",
    )(x_proj, z_proj, b_proj, c_proj, dt_raw)


def conv_silu(value_ref, halo_ref, taps_ref, bias_ref, padded):
    tokens = value_ref.shape[0]
    taps = taps_ref.shape[0]
    padded[0:8, :] = halo_ref[HALO - 8 : HALO, :].astype(jnp.float32)
    padded[8 : 8 + tokens, :] = value_ref[...].astype(jnp.float32)
    total = bias_ref[...] + jnp.zeros(value_ref.shape, jnp.float32)
    for offset in range(taps):
        low = 8 - (taps - 1) + offset
        total = total + taps_ref[offset : offset + 1, :] * padded[low : low + tokens, :]
    return (total / (1.0 + jnp.exp(-total))).astype(jnp.bfloat16)


def local_kernel(
    x_ref,
    b_ref,
    c_ref,
    x_halo,
    b_halo,
    c_halo,
    x_taps,
    x_bias,
    b_taps,
    b_bias,
    c_taps,
    c_bias,
    step_t,
    cum_t,
    cum_c,
    skip_ref,
    y_ref,
    piece_ref,
    final_ref,
    c_out,
    x_pad,
    bc_pad,
    x_t,
    x_w,
    final,
):
    tokens, width = x_ref.shape
    heads = step_t.shape[0]
    blocks = tokens // SPAN
    x_conv = conv_silu(x_ref, x_halo, x_taps, x_bias, x_pad)
    b_conv = conv_silu(b_ref, b_halo, b_taps, b_bias, bc_pad)
    c_conv = conv_silu(c_ref, c_halo, c_taps, c_bias, bc_pad)
    c_out[...] = c_conv
    later = lax.broadcasted_iota(jnp.int32, (SPAN, SPAN), 0)
    earlier = lax.broadcasted_iota(jnp.int32, (SPAN, SPAN), 1)
    causal = later >= earlier
    for block in range(blocks):
        low = block * SPAN
        b_blk = b_conv[low : low + SPAN]
        c_blk = c_conv[low : low + SPAN]
        x_t[...] = x_conv[low : low + SPAN].astype(jnp.float32).T
        scores = lax.dot_general(c_blk, b_blk, NT, preferred_element_type=jnp.float32)
        for head in range(heads):
            rows = pl.ds(head * HEAD_DIM, HEAD_DIM)
            column = cum_c[0, low : low + SPAN, head : head + 1]
            row = cum_t[head : head + 1, low : low + SPAN]
            step = step_t[head : head + 1, low : low + SPAN]
            total = row[:, SPAN - 1 : SPAN]
            decays = jnp.exp(jnp.where(causal, column - row, -jnp.inf))
            mix = (decays * step * scores).astype(jnp.bfloat16)
            x_head = x_t[rows, :]
            product = lax.dot_general(
                x_head.astype(jnp.bfloat16), mix, NT, preferred_element_type=jnp.float32
            )
            y_ref[block, rows, :] = product + skip_ref[0, head : head + 1, :] * x_head
            x_w[rows, :] = (x_head * (step * jnp.exp(total - row))).astype(jnp.bfloat16)
        piece = jnp.dot(x_w[...], b_blk, preferred_element_type=jnp.float32)
        piece_ref[block] = piece
        if block == 0:
            final[...] = piece
        else:
            for head in range(heads):
                rows = pl.ds(head * HEAD_DIM, HEAD_DIM)
                decay = jnp.exp(cum_t[head : head + 1, low + SPAN - 1 : low + SPAN])
                final[rows, :] = decay * final[rows, :] + piece_ref[block, rows, :]
    final_ref[...] = final[...].astype(jnp.bfloat16)


def local_scan(x, b, c, halos, x_taps, x_bias, bc_taps, bc_bias, step_t, cum_t, cum_c, skip):
    tokens, x_cols = x.shape
    groups = b.shape[1] // STATE
    width = x_cols // groups
    heads = width // HEAD_DIM
    blocks = tokens // SPAN
    taps = x_taps.shape[0]

    def cols(rows, size):
        return pl.BlockSpec((rows, size), lambda g: (0, g))

    in_specs = [
        cols(tokens, width),
        cols(tokens, STATE),
        cols(tokens, STATE),
        cols(HALO, width),
        cols(HALO, STATE),
        cols(HALO, STATE),
        cols(taps, width),
        cols(1, width),
        cols(taps, STATE),
        cols(1, STATE),
        cols(taps, STATE),
        cols(1, STATE),
        pl.BlockSpec((heads, tokens), lambda g: (g, 0)),
        pl.BlockSpec((heads, tokens), lambda g: (g, 0)),
        pl.BlockSpec((1, tokens, heads), lambda g: (g, 0, 0)),
        pl.BlockSpec((1, heads, 1), lambda g: (g, 0, 0)),
    ]
    out_specs = [
        pl.BlockSpec((blocks, width, SPAN), lambda g: (0, g, 0)),
        pl.BlockSpec((blocks, width, STATE), lambda g: (0, g, 0)),
        pl.BlockSpec((width, STATE), lambda g: (g, 0)),
        cols(tokens, STATE),
    ]
    out_shape = [
        jax.ShapeDtypeStruct((blocks, x_cols, SPAN), jnp.float32),
        jax.ShapeDtypeStruct((blocks, x_cols, STATE), jnp.float32),
        jax.ShapeDtypeStruct((x_cols, STATE), jnp.bfloat16),
        jax.ShapeDtypeStruct((tokens, groups * STATE), jnp.bfloat16),
    ]
    return pl.pallas_call(
        local_kernel,
        grid=(groups,),
        in_specs=in_specs,
        out_specs=out_specs,
        out_shape=out_shape,
        scratch_shapes=[
            pltpu.VMEM((tokens + 8, width), jnp.float32),
            pltpu.VMEM((tokens + 8, STATE), jnp.float32),
            pltpu.VMEM((width, SPAN), jnp.float32),
            pltpu.VMEM((width, SPAN), jnp.bfloat16),
            pltpu.VMEM((width, STATE), jnp.float32),
        ],
        compiler_params=pltpu.CompilerParams(dimension_semantics=("arbitrary",)),
        cost_estimate=pl.CostEstimate(
            flops=20000000000, bytes_accessed=16000000, transcendentals=4000000
        ),
        name="local_scan",
    )(
        x,
        b,
        c,
        *halos,
        x_taps,
        x_bias[None],
        bc_taps[:, 0],
        bc_bias[0:1],
        bc_taps[:, 1],
        bc_bias[1:2],
        step_t,
        cum_t,
        cum_c,
        skip,
    )


def carry_kernel(start_ref, piece_ref, c_ref, cum_t, y_ref, z_ref, gain_ref, out_ref, running, y_t):
    tokens, width = z_ref.shape
    heads = cum_t.shape[0]
    blocks = tokens // SPAN
    running[...] = start_ref[...].astype(jnp.float32)
    for block in range(blocks):
        low = block * SPAN
        c_blk = c_ref[low : low + SPAN, :]
        carried = lax.dot_general(
            running[...].astype(jnp.bfloat16), c_blk, NT, preferred_element_type=jnp.float32
        )
        y_t[...] = carried
        for head in range(heads):
            rows = pl.ds(head * HEAD_DIM, HEAD_DIM)
            row = jnp.exp(cum_t[head : head + 1, low : low + SPAN])
            y_t[rows, :] = y_ref[block, rows, :] + y_t[rows, :] * row
            if block < blocks - 1:
                running[rows, :] = (
                    row[:, SPAN - 1 : SPAN] * running[rows, :] + piece_ref[block, rows, :]
                )
        gate = z_ref[low : low + SPAN, :].astype(jnp.float32)
        gated = y_t[...].T * (gate / (1.0 + jnp.exp(-gate)))
        mean = jnp.sum(gated * gated, axis=-1, keepdims=True) * (1.0 / width)
        normed = gated * lax.rsqrt(mean + 1.0)
        out_ref[low : low + SPAN, :] = (normed * gain_ref[...]).astype(jnp.bfloat16)


def carry_norm(start, pieces, c_conv, cum_t, y_t, z, gain):
    tokens, x_cols = z.shape
    groups = c_conv.shape[1] // STATE
    width = x_cols // groups
    heads = width // HEAD_DIM
    blocks = tokens // SPAN
    return pl.pallas_call(
        carry_kernel,
        grid=(groups,),
        in_specs=[
            pl.BlockSpec((width, STATE), lambda g: (g, 0)),
            pl.BlockSpec((blocks, width, STATE), lambda g: (0, g, 0)),
            pl.BlockSpec((tokens, STATE), lambda g: (0, g)),
            pl.BlockSpec((heads, tokens), lambda g: (g, 0)),
            pl.BlockSpec((blocks, width, SPAN), lambda g: (0, g, 0)),
            pl.BlockSpec((tokens, width), lambda g: (0, g)),
            pl.BlockSpec((1, width), lambda g: (0, g)),
        ],
        out_specs=pl.BlockSpec((tokens, width), lambda g: (0, g)),
        out_shape=jax.ShapeDtypeStruct((tokens, x_cols), jnp.bfloat16),
        scratch_shapes=[
            pltpu.VMEM((width, STATE), jnp.float32),
            pltpu.VMEM((width, SPAN), jnp.float32),
        ],
        compiler_params=pltpu.CompilerParams(dimension_semantics=("arbitrary",)),
        cost_estimate=pl.CostEstimate(
            flops=5000000000, bytes_accessed=14000000, transcendentals=1000000
        ),
        name="carry_norm",
    )(start, pieces, c_conv, cum_t, y_t, z, gain[None])


def prefix_kernel(count, final_ref, logs_ref, out_ref, pieces, logs, starts, *sems):
    piece_send, piece_recv, log_send, log_recv, start_send, start_recv, own = sems
    seq = lax.axis_index("seq")
    head = lax.axis_index("head")
    rows = pieces.shape[1]
    barrier = pltpu.get_barrier_semaphore()

    def peer_of(step):
        return lax.rem(seq + step, count)

    def part(which):
        return pl.ds(pl.multiple_of(which * rows, 16), rows)

    def remote(source, target, send, recv, peer):
        return pltpu.make_async_remote_copy(
            src_ref=source,
            dst_ref=target,
            send_sem=send,
            recv_sem=recv,
            device_id=(peer, head),
            device_id_type=pl.DeviceIdType.MESH,
        )

    def log_copy(step):
        return remote(
            logs_ref, logs.at[seq], log_send.at[step], log_recv.at[step], peer_of(step)
        )

    def piece_copy(step):
        return remote(
            final_ref.at[part(peer_of(step))],
            pieces.at[seq],
            piece_send.at[step],
            piece_recv.at[step],
            peer_of(step),
        )

    def start_copy(step):
        return remote(
            starts.at[peer_of(step)],
            out_ref.at[part(seq)],
            start_send.at[step],
            start_recv.at[step],
            peer_of(step),
        )

    def each(body):
        def lap(step, carry):
            body(step)
            return carry

        lax.fori_loop(1, count, lap, 0)

    def greet(step):
        pl.semaphore_signal(
            barrier, inc=1, device_id=(peer_of(step), head), device_id_type=pl.DeviceIdType.MESH
        )

    each(greet)
    pl.semaphore_wait(barrier, count - 1)

    def send(step):
        log_copy(step).start()
        piece_copy(step).start()

    each(send)
    own_piece = pltpu.make_async_copy(final_ref.at[part(seq)], pieces.at[seq], own.at[0])
    own_log = pltpu.make_async_copy(logs_ref, logs.at[seq], own.at[1])
    own_piece.start()
    own_log.start()
    own_piece.wait()
    own_log.wait()

    def land(step):
        log_copy(step).wait()
        piece_copy(step).wait()

    each(land)
    per_head = min(rows, HEAD_DIM)
    first = seq * rows // HEAD_DIM
    lanes = logs.shape[2]

    def scan(position, running):
        for index in range(rows // per_head):
            low = index * per_head
            starts[position, low : low + per_head, :] = running[index].astype(jnp.bfloat16)
        decays = jnp.exp(pltpu.roll(logs[position], lax.rem(lanes - first, lanes), 1))
        following = []
        for index in range(rows // per_head):
            low = index * per_head
            piece = pieces[position, low : low + per_head, :].astype(jnp.float32)
            following.append(decays[0:1, index : index + 1] * running[index] + piece)
        return tuple(following)

    zero = jnp.zeros((per_head, pieces.shape[2]), jnp.float32)
    lax.fori_loop(0, count, scan, (zero,) * (rows // per_head))
    each(lambda step: start_copy(step).start())
    own_start = pltpu.make_async_copy(starts.at[seq], out_ref.at[part(seq)], own.at[0])
    own_start.start()
    own_start.wait()
    each(lambda step: start_copy(step).wait())


def carry_in(log_total, final_state):
    count = lax.axis_size("seq")
    total, width = final_state.shape
    rows = total // count
    logs = jnp.broadcast_to(jnp.pad(log_total, (0, 128 - log_total.shape[0]))[None], (8, 128))
    vmem = pl.BlockSpec(memory_space=pltpu.VMEM)
    dma = pltpu.SemaphoreType.DMA
    return pl.pallas_call(
        functools.partial(prefix_kernel, count),
        out_shape=jax.ShapeDtypeStruct(final_state.shape, final_state.dtype),
        in_specs=[vmem, vmem],
        out_specs=vmem,
        scratch_shapes=[
            pltpu.VMEM((count, rows, width), jnp.bfloat16),
            pltpu.VMEM((count, 8, 128), jnp.float32),
            pltpu.VMEM((count, rows, width), jnp.bfloat16),
            dma((count,)),
            dma((count,)),
            dma((count,)),
            dma((count,)),
            dma((count,)),
            dma((count,)),
            dma((2,)),
        ],
        compiler_params=pltpu.CompilerParams(collective_id=1, has_side_effects=True),
        name="prefix_exchange",
    )(final_state, logs)


def per_device(
    x_proj,
    z_proj,
    b_proj,
    c_proj,
    dt_raw,
    dt_bias,
    a_log,
    d_skip,
    conv_x,
    conv_bias_x,
    conv_bc,
    conv_bias_bc,
    norm_weight,
    out_weight,
):
    x_heads, z_heads, b_heads, c_heads, dt_full, *halos = entry_exchange(
        x_proj, z_proj, b_proj, c_proj, dt_raw
    )
    token_count = x_heads.shape[0]
    local_heads = dt_bias.shape[0]
    local_groups = b_heads.shape[1] // STATE
    per_group = local_heads // local_groups
    blocks = token_count // SPAN
    dt_heads = lax.dynamic_slice_in_dim(
        dt_full, lax.axis_index("head") * local_heads, local_heads, axis=1
    )
    step_size = jax.nn.softplus(dt_heads.astype(jnp.float32) + dt_bias)
    rate = (-jnp.exp(a_log) * step_size).reshape(blocks, SPAN, local_heads)
    cumulative = jnp.cumsum(rate, axis=1)
    log_total = jnp.sum(cumulative[:, -1], axis=0)
    cumulative = cumulative.reshape(token_count, local_heads)
    step_t = step_size.T
    cum_t = cumulative.T
    cum_c = jnp.transpose(
        cumulative.reshape(token_count, local_groups, per_group), (1, 0, 2)
    )
    y_t, pieces, final_state, c_conv = local_scan(
        x_heads,
        b_heads,
        c_heads,
        halos,
        conv_x,
        conv_bias_x,
        conv_bc,
        conv_bias_bc,
        step_t,
        cum_t,
        cum_c,
        d_skip.reshape(local_groups, per_group, 1),
    )
    start = carry_in(log_total, final_state)
    normed = carry_norm(start, pieces, c_conv, cum_t, y_t, z_heads, norm_weight)
    terms = jnp.dot(
        normed,
        lax.all_gather(out_weight, "seq", axis=1, tiled=True),
        preferred_element_type=jnp.float32,
    )
    return lax.psum_scatter(terms.astype(jnp.bfloat16), "head", scatter_dimension=0, tiled=True)


def solution(mesh):
    in_specs = (
        P(("seq", "head"), None),
        P(("seq", "head"), None),
        P(("seq", "head"), None),
        P(("seq", "head"), None),
        P(("seq", "head"), None),
        P("head"),
        P("head"),
        P("head"),
        P(None, "head"),
        P("head"),
        P(None, None, "head"),
        P(None, "head"),
        P("head"),
        P("head", "seq"),
    )
    out_specs = P(("seq", "head"), None)
    return jax.shard_map(
        per_device, mesh=mesh, in_specs=in_specs, out_specs=out_specs, check_vma=False
    )
```

time: 324 us -> 288 us (0.89)
  Pallas kernels: 0 us -> 173 us
  local copies, waits for them, and re-layouts: 77.6 us -> 5.5 us
  blocking collectives: 47 us -> 0 us
  other arithmetic: 47.6 us -> 0.96 us
  starting transfers between devices: 37.5 us -> 0.04 us
  matrix products: 28.3 us -> 16.7 us
  waiting for transfers between devices: 66.9 us -> 76.1 us
    pallas_call x0 -> x4, Pallas kernels: none -> 173 us  [the longest x1 77.5 us: carry_in(): pl.pallas_call(functools.partial(prefix_kernel, count), out_shape=jax.Sha...]
    unnamed x1 -> x0, blocking collectives: 47 us -> none
    all_gather x1, waiting for transfers between devices: 0.02 us -> 44.3 us  [per_device(): lax.all_gather(out_weight, 'seq', axis=1, tiled=True)]
    all_to_all x7 -> x0, starting transfers between devices: 35.6 us -> none  [the longest x1 11.3 us: carry_in(): back = lax.all_to_all(jnp.stack(starts), axis, split_axis=0, concat_axis=0)]
    all_to_all x7 -> x0, waiting for transfers between devices: 28.8 us -> none  [the longest x1 20.4 us: per_device(): lax.all_to_all(x_proj, 'head', split_axis=1, concat_axis=0, tiled=True)]
    reshape x7 -> x3, local copies, waits for them, and re-layouts: 29.6 us -> 1.55 us  [the longest x1 0.75 us: per_device(): d_skip.reshape(local_groups, per_group, 1)]
    unnamed x14 -> x0, other arithmetic: 23.1 us -> none
    convert_element_type x10 -> x0, other arithmetic: 19.9 us -> none  [the longest x1 4.53 us: per_device(): (x_blocks.astype(jnp.float32) * state_scale[:, :, :, None]).astype(jnp.bf...]
  transfers between devices with their start and end apart: 10 -> 2, of which waited for: 8 -> 2; matrix products, arithmetic and copies ran while one was open for 42% -> 2% of each run, Pallas kernels for 0% -> 61%
where the time goes in v2:
time: 288 us; the launch traced here: 286 us
  Pallas kernels  173 us (60%)
  waiting for transfers between devices  76.1 us (26%)
  matrix products  16.7 us (6%)
  between operations  13.5 us (5%)
  local copies, waits for them, and re-layouts  5.5 us (2%)
    pallas_call x1, Pallas kernels, carry_in(): pl.pallas_call(functools.partial(prefix_kernel, count), out_shape=jax.Sha...  77.5 us
    pallas_call x1, Pallas kernels, entry_exchange(): pl.pallas_call(functools.partial(entry_kernel, count, heads), out_shape=[...  76.1 us
    all_gather x1, waiting for transfers between devices, per_device(): lax.all_gather(out_weight, 'seq', axis=1, tiled=True)  44.3 us
    reduce_scatter x1, waiting for transfers between devices, per_device(): lax.psum_scatter(terms.astype(jnp.bfloat16), 'head', scatter_dimension=0,...  31.1 us
    dot_general x1, matrix products, per_device(): jnp.dot(normed, lax.all_gather(out_weight, 'seq', axis=1, tiled=True), pr...  16.7 us
    pallas_call x1, Pallas kernels, local_scan(): pl.pallas_call(local_kernel, grid=(groups,), in_specs=in_specs, out_specs...  12 us
    pallas_call x1, Pallas kernels, carry_norm(): pl.pallas_call(carry_kernel, grid=(groups,), in_specs=[pl.BlockSpec((widt...  7.38 us
  transfers between devices with their start and end apart: 2, of which 2 were waited for; matrix products, arithmetic and copies ran while one was open for 2% of the time, Pallas kernels for 61%

profile of v2, /device:TPU:8, one launch (start us, length us, event | category | flops | bytes accessed | tf_op | source)
XLA Modules:
  0.0 285.8 jit_solution(12514449818213551175)
XLA Ops:
  6.5 0.0 all-gather.2.cloned.1.call-start
  6.5 0.7 all-gather.2.cloned.1.call-update
  7.3 0.0 reduce-scatter.2.cloned.1.call-start
  7.3 0.0 copy-start.4
  7.3 0.0 copy-start.2
  7.3 0.0 copy-start.3
  7.3 0.0 copy-start.1
  7.3 0.0 copy-start
  7.4 76.1 %entry_exchange.1 = (bf16[256,4096]{1,0:T(8,128)(2,1)}, bf16[256,4096]{1,0:T(8,128)(2,1)}, bf16[256,512]{1,0:T(8,128)(2,1)}, bf16[256,512]{1,0:T(8,128)(2,1)}, b...) custom-call(bf16[128,8192]{1,0:T(8,128)(2,1)} %refs_0_.1, ...), custom_call_target="tpu_custom_call" | custom-call | tf_op jit(solution)/shard_map/entry_exchange/pallas_call | solution.py:143
  83.5 0.9 copy.23
  84.4 0.0 copy-done.4
  84.4 0.0 copy-done.2
  84.4 0.7 fusion
  85.2 0.1 copy.29
  85.3 0.2 reduce_window_sum.11
  85.5 0.1 copy.26
  85.6 0.7 copy.30
  86.3 0.1 reshape_reshape.3
  86.3 1.0 copy.27
  87.4 0.0 copy-done.3
  87.4 0.8 reshape.15.skip_ref
  88.1 0.0 copy-done.1
  88.1 0.6 fusion.3
  88.7 0.0 copy-done
  88.8 0.6 copy_bitcast_fusion
  89.4 12.0 %local_scan.1 = (f32[2,4096,128]{2,1,0:T(8,128)}, f32[2,4096,128]{2,1,0:T(8,128)}, bf16[4096,128]{1,0:T(8,128)(2,1)}, bf16[256,512]{1,0:T(8,128)(2,1)}) custom-call(bf16[256,4096]{1,0:T(8,128)(2,1)} %get-tuple-element.17.x_ref, bf16[256,512]{1,0:T(8,128)(2,1)} %get-tuple-element.18.b_ref, bf16[256,512]{1,0:T(8,128)(2,1)} %get-tuple-element.19.c_ref, ...), custom_call_target="tpu_custom_call" | custom-call | flops 20000000000 | bytes 16000000 | tf_op jit(solution)/shard_map/local_scan/pallas_call | solution.py:283
  101.4 0.6 broadcast_in_dim.7.logs_ref
  102.0 77.5 %prefix_exchange.1.start_ref = bf16[4096,128]{1,0:T(8,128)(2,1)} custom-call(bf16[4096,128]{1,0:T(8,128)(2,1)} %get-tuple-element.24.final_ref, f32[8,128]{1,0:T(8,128)} %broadcast_in_dim.7.logs_ref), custom_call_target="tpu_custom_call" | custom-call | tf_op jit(solution)/shard_map/prefix_exchange/pallas_call | solution.py:488
  179.5 7.4 %carry_norm.1 = bf16[256,4096]{1,0:T(8,128)(2,1)} custom-call(bf16[4096,128]{1,0:T(8,128)(2,1)} %prefix_exchange.1.start_ref, f32[2,4096,128]{2,1,0:T(8,128)} %get-tuple-element.25.piece_ref, bf16[256,512]{1,0:T(8,128)(2,1)} %get-tuple-element.26.c_ref, f32[64,256]{1,0:T(8,128)} %bitcast.20, f32[2,4096,128]{2,1,0:T(8,128)} %get-tuple-element.27.y_ref, ...), custom_call_target="tpu_custom_call" | custom-call | flops 5000000000 | bytes 14000000 | tf_op jit(solution)/shard_map/carry_norm/pallas_call | solution.py:352
  186.9 44.3 %all-gather.2.cloned.1.call-done = bf16[4096,4096]{1,0:T(8,128)(2,1)} async-done(((bf16[4096,256]{1,0:T(8,128)(2,1)}), bf16[4096,4096]{1,0:T(8,128)(2,1)}) %all-gather.2.cloned.1.call-update) | async-done | bytes 33554448 | tf_op jit(solution)/shard_map/all_gather | solution.py:565
  231.2 16.7 %convolution_convert_fusion = bf16[256,4096]{1,0:T(8,128)(2,1)} fusion(bf16[256,4096]{1,0:T(8,128)(2,1)} %carry_norm.1, bf16[4096,4096]{1,0:T(8,128)(2,1)} %all-gather.2.cloned.1.call-done), kind=kOutput, calls=%fused_computation | convolution fusion | flops 8590983168 | bytes 37748736 | tf_op jit(solution)/shard_map/dot_general | solution.py:563
  247.9 0.0 reduce-scatter.2.cloned.1.call-update
  247.9 31.1 %reduce-scatter.2.cloned.1.call-done = bf16[128,4096]{1,0:T(8,128)(2,1)} async-done(((bf16[256,4096]{1,0:T(8,128)(2,1)}), bf16[128,4096]{1,0:T(8,128)(2,1)}) %reduce-scatter.2.cloned.1.call-update) | async-done | bytes 1048592 | tf_op jit(solution)/shard_map/reduce_scatter | solution.py:568
  (4 shorter events, 0.0 us)
Async XLA Ops:
  6.5 224.6 %all-gather.2.cloned.1.call-start = ((), (), s32[]{:S(2)}) async-start(), calls=%async_computation.1 | async-start | bytes 35651584 | tf_op jit(solution)/shard_map/all_gather | solution.py:565
  7.3 271.7 %reduce-scatter.2.cloned.1.call-start = ((), (), s32[]{:S(2)}) async-start(), calls=%async_computation.2 | async-start | bytes 3145728 | tf_op jit(solution)/shard_map/reduce_scatter | solution.py:568
  7.3 77.1 %copy-start.4 = (f32[64]{0:T(128)S(1)}, f32[64]{0:T(128)}, u32[]{:S(2)}) copy-start(f32[64]{0:T(128)} %param.20) | copy-start | bytes 772
  7.3 77.1 %copy-start.2 = (f32[64]{0:T(128)S(1)}, f32[64]{0:T(128)}, u32[]{:S(2)}) copy-start(f32[64]{0:T(128)} %param.19) | copy-start | bytes 772
  7.3 80.0 %copy-start.3 = (f32[64]{0:T(128)S(1)}, f32[64]{0:T(128)}, u32[]{:S(2)}) copy-start(f32[64]{0:T(128)} %param.21) | copy-start | bytes 772
  7.3 80.8 %copy-start.1 = (f32[2,512]{1,0:T(2,128)S(1)}, f32[2,512]{1,0:T(2,128)}, u32[]{:S(2)}) copy-start(f32[2,512]{1,0:T(2,128)} %param.25) | copy-start | bytes 12292
  7.3 81.4 %copy-start = (f32[4,2,512]{2,1,0:T(2,128)S(1)}, f32[4,2,512]{2,1,0:T(2,128)}, u32[]{:S(2)}) copy-start(f32[4,2,512]{2,1,0:T(2,128)} %param.24) | copy-start | bytes 49156
Sparse Core Ops, SparseCore 0:
  8.8 222.2 all-gather.1
  248.0 30.8 reduce-scatter.1

commit v3 on v2

--- a/solution.py
+++ b/solution.py
@@ -507,6 +507,103 @@
     )(final_state, logs)
 
 
+def project_kernel(
+    heads, normed, weight, out, buffer, terms, landed, load_sems, send_sems, recv_sems
+):
+    seq = lax.axis_index("seq")
+    head = lax.axis_index("head")
+    rows = out.shape[0]
+    tile = buffer.shape[2]
+    tiles = out.shape[1] // tile
+    barrier = pltpu.get_barrier_semaphore()
+    for step in range(1, heads):
+        pl.semaphore_signal(
+            barrier,
+            inc=1,
+            device_id=(seq, lax.rem(head + step, heads)),
+            device_id_type=pl.DeviceIdType.MESH,
+        )
+    pl.semaphore_wait(barrier, heads - 1)
+
+    def load(index):
+        slot = lax.rem(index, 2)
+        return pltpu.make_async_copy(
+            weight.at[:, pl.ds(pl.multiple_of(index * tile, 128), tile)],
+            buffer.at[slot],
+            load_sems.at[slot],
+        )
+
+    def share(index, step):
+        peer = lax.rem(head + step, heads)
+        return pltpu.make_async_remote_copy(
+            src_ref=terms.at[index, pl.ds(pl.multiple_of(peer * rows, 16), rows)],
+            dst_ref=landed.at[index, step - 1],
+            send_sem=send_sems.at[index, step - 1],
+            recv_sem=recv_sems.at[index, step - 1],
+            device_id=(seq, peer),
+            device_id_type=pl.DeviceIdType.MESH,
+        )
+
+    load(0).start()
+
+    def multiply(index, carry):
+        @pl.when(index + 1 < tiles)
+        def _():
+            load(index + 1).start()
+
+        load(index).wait()
+        product = jnp.dot(
+            normed[...], buffer[lax.rem(index, 2)], preferred_element_type=jnp.float32
+        )
+        terms[index] = product.astype(jnp.bfloat16)
+        for step in range(1, heads):
+            share(index, step).start()
+        return carry
+
+    lax.fori_loop(0, tiles, multiply, 0)
+    for index in range(tiles):
+        own = terms[index, pl.ds(pl.multiple_of(head * rows, 16), rows), :]
+        total = own.astype(jnp.float32)
+        for step in range(1, heads):
+            share(index, step).wait()
+            total = total + landed[index, step - 1].astype(jnp.float32)
+        out[:, index * tile : (index + 1) * tile] = total.astype(jnp.bfloat16)
+
+
+def project(normed, weight):
+    heads = lax.axis_size("head")
+    tokens, depth = normed.shape
+    columns = weight.shape[1]
+    rows = tokens // heads
+    tile = min(columns, 256)
+    tiles = columns // tile
+    dma = pltpu.SemaphoreType.DMA
+    return pl.pallas_call(
+        functools.partial(project_kernel, heads),
+        out_shape=jax.ShapeDtypeStruct((rows, columns), jnp.bfloat16),
+        in_specs=[
+            pl.BlockSpec(memory_space=pltpu.VMEM),
+            pl.BlockSpec(memory_space=pl.ANY),
+        ],
+        out_specs=pl.BlockSpec(memory_space=pltpu.VMEM),
+        scratch_shapes=[
+            pltpu.VMEM((2, depth, tile), jnp.bfloat16),
+            pltpu.VMEM((tiles, tokens, tile), jnp.bfloat16),
+            pltpu.VMEM((tiles, heads - 1, rows, tile), jnp.bfloat16),
+            dma((2,)),
+            dma((tiles, heads - 1)),
+            dma((tiles, heads - 1)),
+        ],
+        compiler_params=pltpu.CompilerParams(collective_id=2, has_side_effects=True),
+        cost_estimate=pl.CostEstimate(
+            flops=2 * tokens * depth * columns,
+            bytes_accessed=2 * depth * columns,
+            transcendentals=0,
+        ),
+        name="project",
+    )(normed, weight)
+
+
 def per_device(
     x_proj,
     z_proj,
@@ -560,12 +657,8 @@
     )
     start = carry_in(log_total, final_state)
     normed = carry_norm(start, pieces, c_conv, cum_t, y_t, z_heads, norm_weight)
-    terms = jnp.dot(
-        normed,
-        lax.all_gather(out_weight, "seq", axis=1, tiled=True),
-        preferred_element_type=jnp.float32,
-    )
-    return lax.psum_scatter(terms.astype(jnp.bfloat16), "head", scatter_dimension=0, tiled=True)
+    weight = lax.all_gather(out_weight, "seq", axis=1, tiled=True)
+    return project(normed, weight)
 
 
 def solution(mesh):

time: 288 us -> 274 us (0.951)
  Pallas kernels: 173 us -> 204 us
  waiting for transfers between devices: 76.1 us -> 45.1 us
  matrix products: 16.7 us -> 0 us
    reduce_scatter x1 -> x0, waiting for transfers between devices: 31.1 us -> none  [per_device(): lax.psum_scatter(terms.astype(jnp.bfloat16), 'head', scatter_dimension=0,...]
    pallas_call x0 -> x1, Pallas kernels: none -> 30.5 us  [project(): pl.pallas_call(functools.partial(project_kernel, heads), out_shape=jax.Sh...]
    dot_general x1 -> x0, matrix products: 16.7 us -> none  [per_device(): jnp.dot(normed, lax.all_gather(out_weight, 'seq', axis=1, tiled=True), pr...]
    unnamed x10 -> x12, local copies, waits for them, and re-layouts: 0.02 us -> 2.93 us
  transfers between devices with their start and end apart: 2 -> 1, of which waited for: 2 -> 1; matrix products, arithmetic and copies ran while one was open for 2% -> 2% of each run, Pallas kernels for 61% -> 64%
where the time goes in v3:
time: 274 us; the launch traced here: 271 us
  Pallas kernels  204 us (74%)
  waiting for transfers between devices  45.1 us (16%)
  between operations  13.5 us (5%)
  local copies, waits for them, and re-layouts  7.71 us (3%)
    pallas_call x1, Pallas kernels, carry_in(): pl.pallas_call(functools.partial(prefix_kernel, count), out_shape=jax.Sha...  77.6 us
    pallas_call x1, Pallas kernels, entry_exchange(): pl.pallas_call(functools.partial(entry_kernel, count, heads), out_shape=[...  76.1 us
    all_gather x1, waiting for transfers between devices, per_device(): weight = lax.all_gather(out_weight, 'seq', axis=1, tiled=True)  44.4 us
    pallas_call x1, Pallas kernels, project(): pl.pallas_call(functools.partial(project_kernel, heads), out_shape=jax.Sh...  30.5 us
    pallas_call x1, Pallas kernels, local_scan(): pl.pallas_call(local_kernel, grid=(groups,), in_specs=in_specs, out_specs...  12 us
    pallas_call x1, Pallas kernels, carry_norm(): pl.pallas_call(carry_kernel, grid=(groups,), in_specs=[pl.BlockSpec((widt...  7.38 us
  transfers between devices with their start and end apart: 1, of which 1 were waited for; matrix products, arithmetic and copies ran while one was open for 2% of the time, Pallas kernels for 64%

profile of v3, /device:TPU:8, one launch (start us, length us, event | category | flops | bytes accessed | tf_op | source)
XLA Modules:
  0.0 270.8 jit_solution(8503762614614869061)
XLA Ops:
  6.5 0.0 all-gather.2.cloned.1.call-start
  6.5 0.7 all-gather.2.cloned.1.call-update
  7.3 0.0 copy-start.4
  7.3 0.0 copy-start.2
  7.3 0.0 copy-start.3
  7.3 0.0 copy-start.1
  7.3 0.0 copy-start
  7.3 76.1 %entry_exchange.1 = (bf16[256,4096]{1,0:T(8,128)(2,1)}, bf16[256,4096]{1,0:T(8,128)(2,1)}, bf16[256,512]{1,0:T(8,128)(2,1)}, bf16[256,512]{1,0:T(8,128)(2,1)}, b...) custom-call(bf16[128,8192]{1,0:T(8,128)(2,1)} %refs_0_.1, ...), custom_call_target="tpu_custom_call" | custom-call | tf_op jit(solution)/shard_map/entry_exchange/pallas_call | solution.py:143
  83.4 0.9 copy.23
  84.4 0.0 copy-done.4
  84.4 0.0 copy-done.2
  84.4 0.7 fusion
  85.1 0.1 copy.29
  85.2 0.2 reduce_window_sum.11
  85.4 0.1 copy.25
  85.5 0.1 reshape_reshape.3
  85.6 0.6 copy.36
  86.2 1.0 copy.27
  87.2 0.0 copy-done.3
  87.2 0.8 reshape.15.skip_ref
  88.0 0.0 copy-done.1
  88.0 0.6 fusion.3
  88.6 0.0 copy-done
  88.6 0.6 copy_bitcast_fusion
  89.3 12.0 %local_scan.1 = (f32[2,4096,128]{2,1,0:T(8,128)}, f32[2,4096,128]{2,1,0:T(8,128)}, bf16[4096,128]{1,0:T(8,128)(2,1)}, bf16[256,512]{1,0:T(8,128)(2,1)}) custom-call(bf16[256,4096]{1,0:T(8,128)(2,1)} %get-tuple-element.17.x_ref, bf16[256,512]{1,0:T(8,128)(2,1)} %get-tuple-element.18.b_ref, bf16[256,512]{1,0:T(8,128)(2,1)} %get-tuple-element.19.c_ref, ...), custom_call_target="tpu_custom_call" | custom-call | flops 20000000000 | bytes 16000000 | tf_op jit(solution)/shard_map/local_scan/pallas_call | solution.py:283
  101.2 0.6 broadcast_in_dim.7.logs_ref
  101.8 77.6 %prefix_exchange.1.start_ref = bf16[4096,128]{1,0:T(8,128)(2,1)} custom-call(bf16[4096,128]{1,0:T(8,128)(2,1)} %get-tuple-element.24.final_ref, f32[8,128]{1,0:T(8,128)} %broadcast_in_dim.7.logs_ref), custom_call_target="tpu_custom_call" | custom-call | tf_op jit(solution)/shard_map/prefix_exchange/pallas_call | solution.py:488
  179.4 7.4 %carry_norm.1.normed = bf16[256,4096]{1,0:T(8,128)(2,1)} custom-call(bf16[4096,128]{1,0:T(8,128)(2,1)} %prefix_exchange.1.start_ref, f32[2,4096,128]{2,1,0:T(8,128)} %get-tuple-element.25.piece_ref, bf16[256,512]{1,0:T(8,128)(2,1)} %get-tuple-element.26.c_ref, f32[64,256]{1,0:T(8,128)} %bitcast.25, f32[2,4096,128]{2,1,0:T(8,128)} %get-tuple-element.27.y_ref, ...), custom_call_target="tpu_custom_call" | custom-call | flops 5000000000 | bytes 14000000 | tf_op jit(solution)/shard_map/carry_norm/pallas_call | solution.py:352
  186.8 44.4 %all-gather.2.cloned.1.call-done.weight = bf16[4096,4096]{1,0:T(8,128)(2,1)} async-done(((bf16[4096,256]{1,0:T(8,128)(2,1)}), bf16[4096,4096]{1,0:T(8,128)(2,1)}) %all-gather.2.cloned.1.call-update) | async-done | bytes 33554448 | tf_op jit(solution)/shard_map/all_gather | solution.py:660
  231.2 30.5 %project.1 = bf16[128,4096]{1,0:T(8,128)(2,1)} custom-call(bf16[256,4096]{1,0:T(8,128)(2,1)} %carry_norm.1.normed, bf16[4096,4096]{1,0:T(8,128)(2,1)} %all-gather.2.cloned.1.call-done.weight), custom_call_target="tpu_custom_call" | custom-call | flops 8589934592 | bytes 33554432 | tf_op jit(solution)/shard_map/project/pallas_call | solution.py:581
  261.7 2.3 copy.38
  (4 shorter events, 0.0 us)
Async XLA Ops:
  6.5 224.6 %all-gather.2.cloned.1.call-start = ((), (), s32[]{:S(2)}) async-start(), calls=%async_computation | async-start | bytes 35651584 | tf_op jit(solution)/shard_map/all_gather | solution.py:660
  7.3 77.1 %copy-start.4 = (f32[64]{0:T(128)S(1)}, f32[64]{0:T(128)}, u32[]{:S(2)}) copy-start(f32[64]{0:T(128)} %param.20) | copy-start | bytes 772
  7.3 77.1 %copy-start.2 = (f32[64]{0:T(128)S(1)}, f32[64]{0:T(128)}, u32[]{:S(2)}) copy-start(f32[64]{0:T(128)} %param.19) | copy-start | bytes 772
  7.3 80.0 %copy-start.3 = (f32[64]{0:T(128)S(1)}, f32[64]{0:T(128)}, u32[]{:S(2)}) copy-start(f32[64]{0:T(128)} %param.21) | copy-start | bytes 772
  7.3 80.7 %copy-start.1 = (f32[2,512]{1,0:T(2,128)S(1)}, f32[2,512]{1,0:T(2,128)}, u32[]{:S(2)}) copy-start(f32[2,512]{1,0:T(2,128)} %param.25) | copy-start | bytes 12292
  7.3 81.3 %copy-start = (f32[4,2,512]{2,1,0:T(2,128)S(1)}, f32[4,2,512]{2,1,0:T(2,128)}, u32[]{:S(2)}) copy-start(f32[4,2,512]{2,1,0:T(2,128)} %param.24) | copy-start | bytes 49156
Sparse Core Ops, SparseCore 0:
  8.8 222.2 all-gather.1

commit v4 on v3

--- a/solution.py
+++ b/solution.py
@@ -528,7 +528,7 @@
     def load(index):
         slot = lax.rem(index, 2)
         return pltpu.make_async_copy(
-            weight.at[:, pl.ds(pl.multiple_of(index * tile, 128), tile)],
+            weight.at[index],
             buffer.at[slot],
             load_sems.at[slot],
         )
@@ -573,10 +573,9 @@
 def project(normed, weight):
     heads = lax.axis_size("head")
     tokens, depth = normed.shape
-    columns = weight.shape[1]
+    tiles, _, tile = weight.shape
+    columns = tiles * tile
     rows = tokens // heads
-    tile = min(columns, 256)
-    tiles = columns // tile
     dma = pltpu.SemaphoreType.DMA
     return pl.pallas_call(
         functools.partial(project_kernel, heads),
@@ -657,7 +656,7 @@
     )
     start = carry_in(log_total, final_state)
     normed = carry_norm(start, pieces, c_conv, cum_t, y_t, z_heads, norm_weight)
-    weight = lax.all_gather(out_weight, "seq", axis=1, tiled=True)
+    weight = lax.all_gather(out_weight, "seq")
     return project(normed, weight)
 
 

time: 274 us -> 265 us (0.967)
  waiting for transfers between devices: 45.1 us -> 40.1 us
    all_gather x1, waiting for transfers between devices: 44.4 us -> 39.4 us  [per_device(): weight = lax.all_gather(out_weight, 'seq')]
  transfers between devices with their start and end apart: 1 -> 1, of which waited for: 1 -> 1; matrix products, arithmetic and copies ran while one was open for 2% -> 2% of each run, Pallas kernels for 64% -> 65%
where the time goes in v4:
time: 265 us; the launch traced here: 264 us
  Pallas kernels  202 us (76%)
  waiting for transfers between devices  40.1 us (15%)
  between operations  13.5 us (5%)
  local copies, waits for them, and re-layouts  7.71 us (3%)
    pallas_call x1, Pallas kernels, entry_exchange(): pl.pallas_call(functools.partial(entry_kernel, count, heads), out_shape=[...  76.1 us
    pallas_call x1, Pallas kernels, carry_in(): pl.pallas_call(functools.partial(prefix_kernel, count), out_shape=jax.Sha...  75.8 us
    all_gather x1, waiting for transfers between devices, per_device(): weight = lax.all_gather(out_weight, 'seq')  39.4 us
    pallas_call x1, Pallas kernels, project(): pl.pallas_call(functools.partial(project_kernel, heads), out_shape=jax.Sh...  30.5 us
    pallas_call x1, Pallas kernels, local_scan(): pl.pallas_call(local_kernel, grid=(groups,), in_specs=in_specs, out_specs...  12 us
    pallas_call x1, Pallas kernels, carry_norm(): pl.pallas_call(carry_kernel, grid=(groups,), in_specs=[pl.BlockSpec((widt...  7.38 us
  transfers between devices with their start and end apart: 1, of which 1 were waited for; matrix products, arithmetic and copies ran while one was open for 2% of the time, Pallas kernels for 65%

profile of v4, /device:TPU:8, one launch (start us, length us, event | category | flops | bytes accessed | tf_op | source)
XLA Modules:
  0.0 264.2 jit_solution(12688132750508319992)
XLA Ops:
  6.5 0.0 all-gather.3.cloned.1.call-start
  6.5 0.7 all-gather.3.cloned.1.call-update
  7.3 0.0 copy-start.4
  7.3 0.0 copy-start.2
  7.3 0.0 copy-start.3
  7.3 0.0 copy-start.1
  7.3 0.0 copy-start
  7.3 76.1 %entry_exchange.1 = (bf16[256,4096]{1,0:T(8,128)(2,1)}, bf16[256,4096]{1,0:T(8,128)(2,1)}, bf16[256,512]{1,0:T(8,128)(2,1)}, bf16[256,512]{1,0:T(8,128)(2,1)}, b...) custom-call(bf16[128,8192]{1,0:T(8,128)(2,1)} %refs_0_.1, ...), custom_call_target="tpu_custom_call" | custom-call | tf_op jit(solution)/shard_map/entry_exchange/pallas_call | solution.py:143
  83.4 0.9 copy.23
  84.4 0.0 copy-done.4
  84.4 0.0 copy-done.2
  84.4 0.7 fusion
  85.1 0.1 copy.29
  85.2 0.2 reduce_window_sum.11
  85.4 0.1 copy.25
  85.5 0.1 reshape_reshape.3
  85.6 0.6 copy.36
  86.2 1.0 copy.27
  87.2 0.0 copy-done.3
  87.2 0.8 reshape.16.skip_ref
  88.0 0.0 copy-done.1
  88.0 0.6 fusion.3
  88.6 0.0 copy-done
  88.6 0.6 copy_bitcast_fusion
  89.3 12.0 %local_scan.1 = (f32[2,4096,128]{2,1,0:T(8,128)}, f32[2,4096,128]{2,1,0:T(8,128)}, bf16[4096,128]{1,0:T(8,128)(2,1)}, bf16[256,512]{1,0:T(8,128)(2,1)}) custom-call(bf16[256,4096]{1,0:T(8,128)(2,1)} %get-tuple-element.17.x_ref, bf16[256,512]{1,0:T(8,128)(2,1)} %get-tuple-element.18.b_ref, bf16[256,512]{1,0:T(8,128)(2,1)} %get-tuple-element.19.c_ref, ...), custom_call_target="tpu_custom_call" | custom-call | flops 20000000000 | bytes 16000000 | tf_op jit(solution)/shard_map/local_scan/pallas_call | solution.py:283
  101.3 0.6 broadcast_in_dim.7.logs_ref
  101.9 75.8 %prefix_exchange.1.start_ref = bf16[4096,128]{1,0:T(8,128)(2,1)} custom-call(bf16[4096,128]{1,0:T(8,128)(2,1)} %get-tuple-element.24.final_ref, f32[8,128]{1,0:T(8,128)} %broadcast_in_dim.7.logs_ref), custom_call_target="tpu_custom_call" | custom-call | tf_op jit(solution)/shard_map/prefix_exchange/pallas_call | solution.py:488
  177.7 7.4 %carry_norm.1.normed = bf16[256,4096]{1,0:T(8,128)(2,1)} custom-call(bf16[4096,128]{1,0:T(8,128)(2,1)} %prefix_exchange.1.start_ref, f32[2,4096,128]{2,1,0:T(8,128)} %get-tuple-element.25.piece_ref, bf16[256,512]{1,0:T(8,128)(2,1)} %get-tuple-element.26.c_ref, f32[64,256]{1,0:T(8,128)} %bitcast.27, f32[2,4096,128]{2,1,0:T(8,128)} %get-tuple-element.27.y_ref, ...), custom_call_target="tpu_custom_call" | custom-call | flops 5000000000 | bytes 14000000 | tf_op jit(solution)/shard_map/carry_norm/pallas_call | solution.py:352
  185.1 39.4 %all-gather.3.cloned.1.call-done = bf16[65536,256]{1,0:T(8,128)(2,1)} async-done(((bf16[4096,256]{1,0:T(8,128)(2,1)}), bf16[65536,256]{1,0:T(8,128)(2,1)}) %all-gather.3.cloned.1.call-update) | async-done | bytes 33554448 | tf_op jit(solution)/shard_map/all_gather | solution.py:659
  224.5 30.5 %project.1 = bf16[128,4096]{1,0:T(8,128)(2,1)} custom-call(bf16[256,4096]{1,0:T(8,128)(2,1)} %carry_norm.1.normed, bf16[16,4096,256]{2,1,0:T(8,128)(2,1)} %bitcast.22), custom_call_target="tpu_custom_call" | custom-call | flops 8589934592 | bytes 33554432 | tf_op jit(solution)/shard_map/project/pallas_call | solution.py:580
  255.0 2.3 copy.38
  (4 shorter events, 0.0 us)
Async XLA Ops:
  6.5 218.0 %all-gather.3.cloned.1.call-start = ((), (), s32[]{:S(2)}) async-start(), calls=%async_computation | async-start | bytes 35651584 | tf_op jit(solution)/shard_map/all_gather | solution.py:659
  7.3 77.1 %copy-start.4 = (f32[64]{0:T(128)S(1)}, f32[64]{0:T(128)}, u32[]{:S(2)}) copy-start(f32[64]{0:T(128)} %param.20) | copy-start | bytes 772
  7.3 77.1 %copy-start.2 = (f32[64]{0:T(128)S(1)}, f32[64]{0:T(128)}, u32[]{:S(2)}) copy-start(f32[64]{0:T(128)} %param.19) | copy-start | bytes 772
  7.3 80.0 %copy-start.3 = (f32[64]{0:T(128)S(1)}, f32[64]{0:T(128)}, u32[]{:S(2)}) copy-start(f32[64]{0:T(128)} %param.21) | copy-start | bytes 772
  7.3 80.7 %copy-start.1 = (f32[2,512]{1,0:T(2,128)S(1)}, f32[2,512]{1,0:T(2,128)}, u32[]{:S(2)}) copy-start(f32[2,512]{1,0:T(2,128)} %param.25) | copy-start | bytes 12292
  7.3 81.3 %copy-start = (f32[4,2,512]{2,1,0:T(2,128)S(1)}, f32[4,2,512]{2,1,0:T(2,128)}, u32[]{:S(2)}) copy-start(f32[4,2,512]{2,1,0:T(2,128)} %param.24) | copy-start | bytes 49156
Sparse Core Ops, SparseCore 0:
  8.9 215.5 all-gather.2
